TPU v7x, 1024 devices: a whole 4x8x16 slice. The times are simulated.
1024 devices in a mesh: row: 64 (over z, x), col: 16 (over y, core).
Axes of the slice: x: 4, y: 8, z: 16, core: 2. Of those that a mesh axis runs over, the one named last changes fastest.
Arguments:
- initial_heat: bfloat16 [48, 2048, 4096], P(None, 'row', 'col'), may hold values from -6 to 6
- layer_conductance: bfloat16 [47, 2048, 4096], P(None, 'row', 'col'), may hold values from 0.049804688 to 20
- layer_spacing: float32 [48], replicated, may hold values from 0.5 to 2
- submerged_layers: int32 [2048, 4096], P('row', 'col'), may hold values from 1 to 48
- water_indicator: int32 [2048, 4096], P('row', 'col'), may hold values from 0 to 1, as said below
- seafloor_distance: float32 [2048, 4096], P('row', 'col'), may hold values from 0.5 to 2
Outputs:
- diffused_heat: float32 [48, 2048, 4096], P(None, 'row', 'col')
- height: float32 [2048, 4096], P('row', 'col')
Inputs may be any that keep to these rules, and one draw needn't show every extreme that they name: `water_indicator`: land lies in a few large regions and in scattered single cells.
All inputs are finite; a program needn't handle non-finite values.
Results may differ from a plain program's by a relative error of at most 0.0003.
Values sent between devices are 32-bit elements; how exact they have to be, the bound alone decides.
No kernel may reach another device: no remote copies, remote signals or barrier semaphores. Data moves between devices by JAX's collectives and lax.ppermute only.
A program may use at most 32 MiB of HBM per device.

v0:
```python
import functools
import math

import jax
import jax.numpy as jnp
from jax import lax
from jax.experimental import pallas as pl
from jax.experimental.pallas import tpu as pltpu
from jax.sharding import Mesh
from jax.sharding import PartitionSpec as P

ITERS = 4
CHUNK = 6


def mix_kernel(
    spacing_ref, wet_ref, water_ref, heat_hbm, conduct_hbm, out_hbm, forcing_ref,
    heat_buf, conduct_buf, ratio_buf, value_buf, heat_sem, conduct_sem, out_sem,
):
    levels, rows, cols = heat_buf.shape
    chunks = levels // CHUNK

    def fetch(chunk):
        first = chunk * CHUNK
        count = min(CHUNK, levels - 1 - first)
        return (
            pltpu.make_async_copy(
                heat_hbm.at[pl.ds(first, CHUNK)], heat_buf.at[pl.ds(first, CHUNK)], heat_sem.at[chunk]
            ),
            pltpu.make_async_copy(
                conduct_hbm.at[pl.ds(first, count)], conduct_buf.at[pl.ds(first, count)], conduct_sem.at[chunk]
            ),
        )

    def flush(chunk):
        first = chunk * CHUNK
        return pltpu.make_async_copy(
            value_buf.at[pl.ds(first, CHUNK)], out_hbm.at[pl.ds(first, CHUNK)], out_sem.at[chunk]
        )

    for chunk in range(chunks):
        for copy in fetch(chunk):
            copy.start()
    wet = wet_ref[...]
    zero = jnp.zeros((rows, cols), jnp.float32)

    def down(level, carry, last=False):
        couple_prev, ratio_prev, value_prev = carry
        spacing = spacing_ref[level]
        if last:
            couple = zero
        else:
            couple = jnp.where(level + 1 < wet, conduct_buf[level].astype(jnp.float32), 0.0)
        source = spacing * heat_buf[level].astype(jnp.float32)
        pivot = spacing + couple_prev + couple - couple_prev * ratio_prev
        inverse = 1.0 / pivot
        ratio = couple * inverse
        value = (source + couple_prev * value_prev) * inverse
        ratio_buf[level] = ratio
        value_buf[level] = value
        return couple, ratio, value

    carry = (zero, zero, zero)
    for chunk in range(chunks):
        for copy in fetch(chunk):
            copy.wait()
        first = chunk * CHUNK
        stop = min(first + CHUNK, levels - 1)
        carry = lax.fori_loop(first, stop, down, carry)
    carry = down(levels - 1, carry, last=True)

    def up(step, carry, first):
        below, total = carry
        level = first + CHUNK - 1 - step
        result = value_buf[level] + ratio_buf[level] * below
        value_buf[level] = result
        total = total + jnp.where(level < wet, spacing_ref[level] * result, 0.0)
        return result, total

    carry = (zero, zero)
    for chunk in reversed(range(chunks)):
        carry = lax.fori_loop(0, CHUNK, functools.partial(up, first=chunk * CHUNK), carry)
        flush(chunk).start()
    forcing_ref[...] = water_ref[...].astype(jnp.float32) * carry[1] * (1.0 / math.sqrt(levels))
    for chunk in reversed(range(chunks)):
        flush(chunk).wait()


def mix(heat, conduct, spacing, wet, water):
    levels, rows, cols = heat.shape
    chunks = levels // CHUNK
    vmem = pl.BlockSpec(memory_space=pltpu.VMEM)
    hbm = pl.BlockSpec(memory_space=pl.ANY)
    return pl.pallas_call(
        mix_kernel,
        in_specs=[pl.BlockSpec(memory_space=pltpu.SMEM), vmem, vmem, hbm, hbm],
        out_specs=[hbm, vmem],
        out_shape=[
            jax.ShapeDtypeStruct((levels, rows, cols), jnp.float32),
            jax.ShapeDtypeStruct((rows, cols), jnp.float32),
        ],
        scratch_shapes=[
            pltpu.VMEM((levels, rows, cols), heat.dtype),
            pltpu.VMEM((levels, rows, cols), conduct.dtype),
            pltpu.VMEM((levels, rows, cols), jnp.float32),
            pltpu.VMEM((levels, rows, cols), jnp.float32),
            pltpu.SemaphoreType.DMA((chunks,)),
            pltpu.SemaphoreType.DMA((chunks,)),
            pltpu.SemaphoreType.DMA((chunks,)),
        ],
        name="mix",
    )(spacing, wet, water, heat, conduct)


ROW = ("row_0", "row_1")
COL = ("col_0", "col_1")
HALO = ITERS
VMEM = pl.BlockSpec(memory_space=pltpu.VMEM)
surface_term = 0.5


def rows_kernel(forcing_ref, depth_ref, water_ref, north_ref, south_ref):
    rows = forcing_ref.shape[0]
    for slot, field in enumerate((forcing_ref[...], depth_ref[...], water_ref[...].astype(jnp.float32))):
        north_ref[slot * HALO : (slot + 1) * HALO] = field[:HALO]
        south_ref[slot * HALO : (slot + 1) * HALO] = field[rows - HALO :]


def edge_kernel(forcing_ref, depth_ref, water_ref, north_ref, south_ref, tall_ref, edge_ref):
    rows, cols = forcing_ref.shape
    tall = rows + 2 * HALO
    lane = lax.broadcasted_iota(jnp.int32, (tall, 128), 1)
    for slot, field in enumerate((forcing_ref[...], depth_ref[...], water_ref[...].astype(jnp.float32))):
        tall_ref[slot, :rows] = field
        tall_ref[slot, rows : rows + HALO] = south_ref[slot * HALO : (slot + 1) * HALO]
        tall_ref[slot, rows + HALO :] = north_ref[slot * HALO : (slot + 1) * HALO]
        edge_ref[slot] = jnp.where(lane < 64, tall_ref[slot, :, :128], tall_ref[slot, :, cols - 128 :])


def around(field):
    tall, wide = field.shape
    beside = pltpu.roll(field, 1, 0) + pltpu.roll(field, tall - 1, 0)
    slant = field + 0.5 * beside
    return beside + (pltpu.roll(slant, 1, 1) + pltpu.roll(slant, wide - 1, 1))


def weights_kernel(tall_ref, west_ref, east_ref, wide_ref, centre_ref, bound_ref):
    tall, cols = tall_ref.shape[1:]
    rows = tall - 2 * HALO
    lane = lax.broadcasted_iota(jnp.int32, (tall, 128), 1)
    full = []
    for slot in range(3):
        side = jnp.where(lane < HALO, east_ref[slot], jnp.where(lane >= 128 - HALO, west_ref[slot], 0.0))
        full.append(jnp.concatenate([tall_ref[slot], side], axis=1))
    forcing, depth, ocean = full
    wet_depth = depth * ocean
    centre = surface_term + 0.5 * (wet_depth * around(ocean) + ocean * around(wet_depth))
    wide_ref[0] = forcing
    wide_ref[1] = wet_depth
    wide_ref[2] = ocean
    centre_ref[...] = centre
    own = 2.0 * centre[:rows, :cols] - surface_term
    high = jnp.max(jnp.max(own, axis=0, keepdims=True), axis=1, keepdims=True)
    bound_ref[...] = jnp.broadcast_to(high, bound_ref.shape)


def solve_kernel(bound_ref, wide_ref, centre_ref, height_ref):
    rows, cols = height_ref.shape
    tall, wide = centre_ref.shape
    top = jnp.max(bound_ref[...], axis=0, keepdims=True)
    top = jnp.concatenate([top] * (wide // 128), axis=1)
    theta = 0.5 * (top + surface_term)
    delta = 0.5 * (top - surface_term)
    sigma = theta / delta
    wet_depth, ocean, centre = wide_ref[1], wide_ref[2], centre_ref[...]
    residual = wide_ref[0]
    direction = residual / theta
    total = direction
    recur = 1.0 / sigma
    for step in range(ITERS):
        image = centre * direction - 0.5 * (
            wet_depth * around(ocean * direction) + ocean * around(wet_depth * direction)
        )
        residual = residual - image
        recur_next = 1.0 / (2.0 * sigma - recur)
        direction = (recur_next * recur) * direction + (2.0 * recur_next / delta) * residual
        recur = recur_next
        total = total + direction
    height_ref[...] = total[:rows, :cols]


def call(kernel, outs, *args):
    shapes = [jax.ShapeDtypeStruct(shape, jnp.float32) for shape in outs]
    return pl.pallas_call(
        kernel, in_specs=[VMEM] * len(args), out_specs=[VMEM] * len(outs), out_shape=shapes, name=kernel.__name__
    )(*args)


def local(heat, conduct, spacing, wet, water, depth):
    rows, cols = depth.shape
    tall, wide = rows + 2 * HALO, cols + 128
    devices = lax.axis_size(ROW) * lax.axis_size(COL)
    diffused, forcing = mix(heat, conduct, spacing, wet, water)
    to_north, to_south = call(rows_kernel, [(3 * HALO, cols)] * 2, forcing, depth, water)
    down = [(i, i + 1) for i in range(lax.axis_size(ROW) - 1)]
    north = lax.ppermute(to_south, ROW, down)
    south = lax.ppermute(to_north, ROW, [(b, a) for a, b in down])
    fields, edge = call(edge_kernel, [(3, tall, cols), (3, tall, 128)], forcing, depth, water, north, south)
    ring = [(i, (i + 1) % lax.axis_size(COL)) for i in range(lax.axis_size(COL))]
    west = lax.ppermute(edge, COL, ring)
    east = lax.ppermute(edge, COL, [(b, a) for a, b in ring])
    full, centre, bound = call(
        weights_kernel, [(3, tall, wide), (tall, wide), (devices, 128)], fields, west, east
    )
    bounds = lax.all_to_all(bound, ROW + COL, 0, 0, tiled=True)
    (height,) = call(solve_kernel, [(rows, cols)], bounds, full, centre)
    return diffused, height


def solution(mesh):
    torus = Mesh(mesh.devices.reshape(16, 4, 8, 2), ROW + COL)
    return jax.shard_map(
        local,
        mesh=torus,
        in_specs=(P(None, ROW, COL), P(None, ROW, COL), P(), P(ROW, COL), P(ROW, COL), P(ROW, COL)),
        out_specs=(P(None, ROW, COL), P(ROW, COL)),
        check_vma=False,
    )
```

profile of v0, /device:TPU:1, one launch (start us, length us, event | category | flops | bytes accessed | tf_op | source)
XLA Modules:
  0.0 102.3 jit_solution(7002529892732532244)
XLA Ops:
  0.6 4.9 %mix.1 = (f32[48,32,256]{2,1,0:T(8,128)}, f32[32,256]{1,0:T(8,128)}) custom-call(f32[48]{0:T(128)} %spacing_ref.1, s32[32,256]{1,0:T(8,128)} %wet_ref.1, s32[32,256]{1,0:T(8,128)} %water_ref.5, bf16[48,32,256]{2,1,0:T(8,128)(2,1)} %heat_hbm.1, bf16[47,32,256]{2,1,0:T(8,128)(2,1)} %conduct_hbm.1), custom_call_target="tpu_custom_call" | custom-call | tf_op jit(solution)/shard_map/mix/pallas_call | solution.py:94
  5.6 1.4 %rows_kernel.1 = (f32[12,256]{1,0:T(8,128)}, f32[12,256]{1,0:T(8,128)}) custom-call(f32[32,256]{1,0:T(8,128)} %get-tuple-element.12.forcing_ref, f32[32,256]{1,0:T(8,128)} %depth_ref.3, s32[32,256]{1,0:T(8,128)} %water_ref.5), custom_call_target="tpu_custom_call" | custom-call | tf_op jit(solution)/shard_map/rows_kernel/pallas_call | solution.py:194
  7.0 3.9 %collective-permute-start = (f32[12,256]{1,0:T(8,128)}, f32[12,256]{1,0:T(8,128)S(1)}, u32[]{:S(2)}, u32[]{:S(2)}) collective-permute-start(f32[12,256]{1,0:T(8,128)} %get-tuple-element.13), channel_id=1, source_target_pairs={{0,16},{16,32},{32,48},{48,64},{64,80},{80,96},{96,112},{112,128},... | collective-permute-start | bytes 36872 | tf_op jit(solution)/shard_map/ppermute | solution.py:206
  10.9 1.3 %collective-permute-start.1 = (f32[12,256]{1,0:T(8,128)}, f32[12,256]{1,0:T(8,128)S(1)}, u32[]{:S(2)}, u32[]{:S(2)}) collective-permute-start(f32[12,256]{1,0:T(8,128)} %get-tuple-element.14), channel_id=1, source_target_pairs={{16,0},{32,16},{48,32},{64,48},{80,64},{96,80},{112,96},{128,112},... | collective-permute-start | bytes 36872 | tf_op jit(solution)/shard_map/ppermute | solution.py:207
  12.2 0.0 collective-permute-done.north_ref
  12.2 0.0 copy-start.2
  12.2 3.4 %collective-permute-done.1.south_ref = f32[12,256]{1,0:T(8,128)S(1)} collective-permute-done((f32[12,256]{1,0:T(8,128)}, f32[12,256]{1,0:T(8,128)S(1)}, u32[]{:S(2)}, u32[]{:S(2)}) %collective-permute-start.1) | collective-permute-done | bytes 12320 | tf_op jit(solution)/shard_map/ppermute | solution.py:207
  15.6 0.0 copy-done.2
  15.6 0.0 copy-start.3
  15.6 0.6 copy-done.3
  16.2 1.5 %edge_kernel.1 = (f32[3,40,256]{2,1,0:T(8,128)}, f32[3,40,128]{2,1,0:T(8,128)}) custom-call(f32[32,256]{1,0:T(8,128)} %get-tuple-element.12.forcing_ref, f32[32,256]{1,0:T(8,128)} %depth_ref.3, s32[32,256]{1,0:T(8,128)} %water_ref.5, f32[12,256]{1,0:T(8,128)} %copy-done.2, f32[12,256]{1,0:T(8,128)} %copy-done.3), custom_call_target="tpu_custom_call" | custom-call | tf_op jit(solution)/shard_map/edge_kernel/pallas_call | solution.py:194
  17.7 12.6 %collective-permute-start.3 = (f32[3,40,128]{2,1,0:T(8,128)}, f32[3,40,128]{2,1,0:T(8,128)S(1)}, u32[]{:S(2)}, u32[]{:S(2)}) collective-permute-start(f32[3,40,128]{2,1,0:T(8,128)} %get-tuple-element.16), channel_id=1, source_target_pairs={{1,0},{2,1},{3,2},{4,3},{5,4},{6,5},{7,6},{8,7},{9,8},{10,9},{11,1... | collective-permute-start | bytes 184328 | tf_op jit(solution)/shard_map/ppermute | solution.py:211
  30.3 0.0 collective-permute-start.2
  30.3 1.1 %collective-permute-done.3.east_ref = f32[3,40,128]{2,1,0:T(8,128)S(1)} collective-permute-done((f32[3,40,128]{2,1,0:T(8,128)}, f32[3,40,128]{2,1,0:T(8,128)S(1)}, u32[]{:S(2)}, u32[]{:S(2)}) %collective-permute-start.3) | collective-permute-done | bytes 61472 | tf_op jit(solution)/shard_map/ppermute | solution.py:211
  31.4 0.0 copy-start
  31.4 0.5 collective-permute-done.2.west_ref
  31.9 0.0 copy-start.1
  31.9 0.1 copy-done
  32.0 0.5 copy-done.1
  32.5 2.0 %weights_kernel.1 = (f32[3,40,384]{2,1,0:T(8,128)}, f32[40,384]{1,0:T(8,128)}, f32[1024,128]{1,0:T(8,128)}) custom-call(f32[3,40,256]{2,1,0:T(8,128)} %get-tuple-element.15.tall_ref, f32[3,40,128]{2,1,0:T(8,128)} %copy-done.1, f32[3,40,128]{2,1,0:T(8,128)} %copy-done), custom_call_target="tpu_custom_call" | custom-call | tf_op jit(solution)/shard_map/weights_kernel/pallas_call | solution.py:194
  34.5 65.3 %all_to_all.11 = f32[1024,1,128]{2,1,0:T(1,128)} all-to-all(f32[1024,1,128]{2,1,0:T(1,128)} %bitcast.5), channel_id=1, replica_groups=mesh['row_0'=16,'row_1'=4,'col_0'=8,'col_1'=2] {'row_0','row_1','col_0',..., dimensions={0} | all-to-all | bytes 1048576 | tf_op jit(solution)/shard_map/all_to_all | solution.py:215
  99.9 2.5 %solve_kernel.1 = f32[32,256]{1,0:T(8,128)} custom-call(f32[1024,128]{1,0:T(8,128)} %bitcast.4, f32[3,40,384]{2,1,0:T(8,128)} %get-tuple-element.18.wide_ref, f32[40,384]{1,0:T(8,128)} %get-tuple-element.19.centre_ref), custom_call_target="tpu_custom_call" | custom-call | tf_op jit(solution)/shard_map/solve_kernel/pallas_call | solution.py:194
Async XLA Ops:
  7.0 5.2 %collective-permute-start = (f32[12,256]{1,0:T(8,128)}, f32[12,256]{1,0:T(8,128)S(1)}, u32[]{:S(2)}, u32[]{:S(2)}) collective-permute-start(f32[12,256]{1,0:T(8,128)} %get-tuple-element.13), channel_id=1, source_target_pairs={{0,16},{16,32},{32,48},{48,64},{64,80},{80,96},{96,112},{112,128},... | collective-permute-start | bytes 36872 | tf_op jit(solution)/shard_map/ppermute | solution.py:206
  10.9 4.7 %collective-permute-start.1 = (f32[12,256]{1,0:T(8,128)}, f32[12,256]{1,0:T(8,128)S(1)}, u32[]{:S(2)}, u32[]{:S(2)}) collective-permute-start(f32[12,256]{1,0:T(8,128)} %get-tuple-element.14), channel_id=1, source_target_pairs={{16,0},{32,16},{48,32},{64,48},{80,64},{96,80},{112,96},{128,112},... | collective-permute-start | bytes 36872 | tf_op jit(solution)/shard_map/ppermute | solution.py:207
  12.2 3.4 %copy-start.2 = (f32[12,256]{1,0:T(8,128)}, f32[12,256]{1,0:T(8,128)S(1)}, u32[]{:S(2)}) copy-start(f32[12,256]{1,0:T(8,128)S(1)} %collective-permute-done.north_ref) | copy-start | bytes 36868
  15.6 0.6 copy-start.3
  17.7 13.7 %collective-permute-start.3 = (f32[3,40,128]{2,1,0:T(8,128)}, f32[3,40,128]{2,1,0:T(8,128)S(1)}, u32[]{:S(2)}, u32[]{:S(2)}) collective-permute-start(f32[3,40,128]{2,1,0:T(8,128)} %get-tuple-element.16), channel_id=1, source_target_pairs={{1,0},{2,1},{3,2},{4,3},{5,4},{6,5},{7,6},{8,7},{9,8},{10,9},{11,1... | collective-permute-start | bytes 184328 | tf_op jit(solution)/shard_map/ppermute | solution.py:211
  30.3 1.6 %collective-permute-start.2 = (f32[3,40,128]{2,1,0:T(8,128)}, f32[3,40,128]{2,1,0:T(8,128)S(1)}, u32[]{:S(2)}, u32[]{:S(2)}) collective-permute-start(f32[3,40,128]{2,1,0:T(8,128)} %get-tuple-element.16), channel_id=1, source_target_pairs={{0,1},{1,2},{2,3},{3,4},{4,5},{5,6},{6,7},{7,8},{8,9},{9,10},{10,1... | collective-permute-start | bytes 184328 | tf_op jit(solution)/shard_map/ppermute | solution.py:210
  31.4 0.6 copy-start
  31.9 0.6 copy-start.1
where the time goes:
time: 103 us; the launch traced here: 102 us
  blocking collectives  65.3 us (63%)
  starting transfers between devices  17.8 us (17%)
  Pallas kernels  12.3 us (12%)
  waiting for transfers between devices  4.98 us (5%)
  local copies, waits for them, and re-layouts  1.22 us (1%)
    all_to_all x1, blocking collectives, local(): bounds = lax.all_to_all(bound, ROW + COL, 0, 0, tiled=True)  65.3 us
    ppermute x1, starting transfers between devices, local(): east = lax.ppermute(edge, COL, [(b, a) for a, b in ring])  12.6 us
    pallas_call x4, Pallas kernels, call(): pl.pallas_call(kernel, in_specs=[VMEM] * len(args), out_specs=[VMEM] * le...  7.36 us
    pallas_call x1, Pallas kernels, mix(): pl.pallas_call(mix_kernel, in_specs=[pl.BlockSpec(memory_space=pltpu.SMEM...  4.92 us
    ppermute x1, starting transfers between devices, local(): north = lax.ppermute(to_south, ROW, down)  3.92 us
    ppermute x1, waiting for transfers between devices, local(): south = lax.ppermute(to_north, ROW, [(b, a) for a, b in down])  3.37 us
  transfers between devices with their start and end apart: 4, of which 3 were waited for; matrix products, arithmetic and copies ran while one was open for 0% of the time, Pallas kernels for 0%

commit v1 on v0

v1 whole, which is shorter than its diff:
```python
import functools
import math

import jax
import jax.numpy as jnp
from jax import lax
from jax.experimental import pallas as pl
from jax.experimental.pallas import tpu as pltpu
from jax.sharding import Mesh
from jax.sharding import PartitionSpec as P

ITERS = 4
CHUNK = 6
ROW = ("row_0", "row_1")
COL = ("col_0", "col_1")
HALO = ITERS
VMEM = pl.BlockSpec(memory_space=pltpu.VMEM)
SMEM = pl.BlockSpec(memory_space=pltpu.SMEM)
surface_term = 0.5


def mix_kernel(
    spacing_ref, wet_hbm, water_hbm, depth_hbm, heat_hbm, conduct_hbm,
    out_hbm, forcing_hbm, north_hbm, south_hbm,
    forcing_ref, north_ref, south_ref, wet_ref, water_ref, depth_ref, heat_buf, conduct_buf, ratio_buf, value_buf,
    plane_sem, edge_sem, heat_sem, conduct_sem, out_sem,
):
    levels, rows, cols = heat_buf.shape
    chunks = levels // CHUNK
    planes = [
        pltpu.make_async_copy(source, target, plane_sem.at[slot])
        for slot, (source, target) in enumerate(
            ((wet_hbm, wet_ref), (water_hbm, water_ref), (depth_hbm, depth_ref))
        )
    ]
    planes[0].start()

    def fetch(chunk):
        first = chunk * CHUNK
        count = min(CHUNK, levels - 1 - first)
        return (
            pltpu.make_async_copy(
                heat_hbm.at[pl.ds(first, CHUNK)], heat_buf.at[pl.ds(first, CHUNK)], heat_sem.at[chunk]
            ),
            pltpu.make_async_copy(
                conduct_hbm.at[pl.ds(first, count)], conduct_buf.at[pl.ds(first, count)], conduct_sem.at[chunk]
            ),
        )

    def flush(chunk):
        first = chunk * CHUNK
        return pltpu.make_async_copy(
            value_buf.at[pl.ds(first, CHUNK)], out_hbm.at[pl.ds(first, CHUNK)], out_sem.at[chunk]
        )

    for chunk in range(chunks):
        for copy in fetch(chunk):
            copy.start()
    planes[1].start()
    planes[2].start()
    planes[0].wait()
    wet = wet_ref[...]
    zero = jnp.zeros((rows, cols), jnp.float32)

    def down(level, carry, last=False):
        couple_prev, ratio_prev, value_prev = carry
        spacing = spacing_ref[level]
        if last:
            couple = zero
        else:
            couple = jnp.where(level + 1 < wet, conduct_buf[level].astype(jnp.float32), 0.0)
        source = spacing * heat_buf[level].astype(jnp.float32)
        pivot = spacing + couple_prev + couple - couple_prev * ratio_prev
        inverse = 1.0 / pivot
        ratio = couple * inverse
        value = (source + couple_prev * value_prev) * inverse
        ratio_buf[level] = ratio
        value_buf[level] = value
        return couple, ratio, value

    carry = (zero, zero, zero)
    for chunk in range(chunks):
        for copy in fetch(chunk):
            copy.wait()
        first = chunk * CHUNK
        stop = min(first + CHUNK, levels - 1)
        carry = lax.fori_loop(first, stop, down, carry)
    carry = down(levels - 1, carry, last=True)

    def up(step, carry, first):
        below, total = carry
        level = first + CHUNK - 1 - step
        result = value_buf[level] + ratio_buf[level] * below
        value_buf[level] = result
        total = total + jnp.where(level < wet, spacing_ref[level] * result, 0.0)
        return result, total

    carry = (zero, zero)
    for chunk in reversed(range(chunks)):
        carry = lax.fori_loop(0, CHUNK, functools.partial(up, first=chunk * CHUNK), carry)
        flush(chunk).start()
    planes[1].wait()
    planes[2].wait()
    ocean = water_ref[...].astype(jnp.float32)
    forcing = ocean * carry[1] * (1.0 / math.sqrt(levels))
    forcing_ref[...] = forcing
    for slot, field in enumerate((forcing, depth_ref[...], ocean)):
        north_ref[slot * HALO : (slot + 1) * HALO] = field[:HALO]
        south_ref[slot * HALO : (slot + 1) * HALO] = field[rows - HALO :]
    edges = [
        pltpu.make_async_copy(source, target, edge_sem.at[slot])
        for slot, (source, target) in enumerate(
            ((north_ref, north_hbm), (south_ref, south_hbm), (forcing_ref, forcing_hbm))
        )
    ]
    for copy in edges:
        copy.start()
    for chunk in reversed(range(chunks)):
        flush(chunk).wait()
    for copy in edges:
        copy.wait()


def mix(heat, conduct, spacing, wet, water, depth):
    levels, rows, cols = heat.shape
    chunks = levels // CHUNK
    hbm = pl.BlockSpec(memory_space=pltpu.HBM)
    return pl.pallas_call(
        mix_kernel,
        in_specs=[pl.BlockSpec(memory_space=pltpu.SMEM), hbm, hbm, hbm, hbm, hbm],
        out_specs=[hbm, hbm, hbm, hbm],
        out_shape=[
            jax.ShapeDtypeStruct((levels, rows, cols), jnp.float32),
            jax.ShapeDtypeStruct((rows, cols), jnp.float32),
            jax.ShapeDtypeStruct((3 * HALO, cols), jnp.float32),
            jax.ShapeDtypeStruct((3 * HALO, cols), jnp.float32),
        ],
        scratch_shapes=[
            pltpu.VMEM((rows, cols), jnp.float32),
            pltpu.VMEM((3 * HALO, cols), jnp.float32),
            pltpu.VMEM((3 * HALO, cols), jnp.float32),
            pltpu.VMEM((rows, cols), wet.dtype),
            pltpu.VMEM((rows, cols), water.dtype),
            pltpu.VMEM((rows, cols), depth.dtype),
            pltpu.VMEM((levels, rows, cols), heat.dtype),
            pltpu.VMEM((levels, rows, cols), conduct.dtype),
            pltpu.VMEM((levels, rows, cols), jnp.float32),
            pltpu.VMEM((levels, rows, cols), jnp.float32),
            pltpu.SemaphoreType.DMA((3,)),
            pltpu.SemaphoreType.DMA((3,)),
            pltpu.SemaphoreType.DMA((chunks,)),
            pltpu.SemaphoreType.DMA((chunks,)),
            pltpu.SemaphoreType.DMA((chunks,)),
        ],
        name="mix",
    )(spacing, wet, water, depth, heat, conduct)


def around(field):
    tall, wide = field.shape
    beside = pltpu.roll(field, 1, 0) + pltpu.roll(field, tall - 1, 0)
    slant = field + 0.5 * beside
    return beside + (pltpu.roll(slant, 1, 1) + pltpu.roll(slant, wide - 1, 1))


def centre_of(wet_depth, ocean):
    return surface_term + 0.5 * (wet_depth * around(ocean) + ocean * around(wet_depth))


def most(field):
    return jnp.max(jnp.max(field, axis=0, keepdims=True), axis=1, keepdims=True)


def edge_kernel(forcing_ref, depth_ref, water_ref, north_ref, south_ref, tall_ref, slots_ref, pack_ref):
    rows, cols = forcing_ref.shape
    tall = rows + 2 * HALO
    lane = lax.broadcasted_iota(jnp.int32, (tall, 128), 1)
    for slot, field in enumerate((forcing_ref[...], depth_ref[...], water_ref[...].astype(jnp.float32))):
        tall_ref[slot, :HALO] = north_ref[slot * HALO : (slot + 1) * HALO]
        tall_ref[slot, HALO : HALO + rows] = field
        tall_ref[slot, HALO + rows :] = south_ref[slot * HALO : (slot + 1) * HALO]
        pack_ref[slot * tall : (slot + 1) * tall] = jnp.where(
            lane < 64, tall_ref[slot, :, :128], tall_ref[slot, :, cols - 128 :]
        )
    ocean = tall_ref[2]
    centre = centre_of(tall_ref[1] * ocean, ocean)
    row = lax.broadcasted_iota(jnp.int32, (tall, cols), 0)
    col = lax.broadcasted_iota(jnp.int32, (tall, cols), 1)
    inner = (row >= HALO) & (row < HALO + rows) & (col >= 1) & (col < cols - 1)
    pack_ref[3 * tall :] = jnp.broadcast_to(most(jnp.where(inner, centre, 0.0)), (128 - 3 * tall, 128))
    turned = pack_ref[...].T
    which = lax.broadcasted_iota(jnp.int32, (8, 128), 0)
    tile = jnp.where(which < HALO, turned[:8], turned[120:])
    for slot in range(slots_ref.shape[0] // 8):
        slots_ref[slot * 8 : (slot + 1) * 8] = tile


def weights_kernel(index_ref, slots_ref, tall_ref, wide_ref, centre_ref, bound_ref, pack_ref):
    tall, cols = tall_ref.shape[1:]
    devices = slots_ref.shape[0] // 8
    index = index_ref[0]
    which = lax.broadcasted_iota(jnp.int32, (8, 128), 0)
    east = slots_ref[pl.ds(pl.multiple_of(lax.rem(index + 1, devices) * 8, 8), 8)]
    west = slots_ref[pl.ds(pl.multiple_of(lax.rem(index + devices - 1, devices) * 8, 8), 8)]
    pack_ref[...] = jnp.zeros((128, 128), jnp.float32)
    pack_ref[:8] = jnp.where(which < HALO, east, 0.0)
    pack_ref[120:] = jnp.where(which >= HALO, west, 0.0)
    turned = pack_ref[...].T
    forcing, depth, ocean = (
        jnp.concatenate([tall_ref[slot], turned[slot * tall : (slot + 1) * tall]], axis=1) for slot in range(3)
    )
    wet_depth = depth * ocean
    wide_ref[0] = forcing
    wide_ref[1] = wet_depth
    wide_ref[2] = ocean
    centre_ref[...] = centre_of(wet_depth, ocean)
    slots = slots_ref[...]
    joint = pltpu.roll(slots, HALO, 0)
    joint_ocean = pltpu.roll(joint, 128 - tall, 1)
    joint_centre = centre_of(joint * joint_ocean, joint_ocean)
    row = lax.broadcasted_iota(jnp.int32, joint.shape, 0) % 8
    lane = lax.broadcasted_iota(jnp.int32, joint.shape, 1)
    seam = ((row == HALO - 1) | (row == HALO)) & (lane >= tall + HALO) & (lane < 2 * tall - HALO)
    high = most(jnp.where(seam, joint_centre, jnp.where(lane >= 3 * tall, slots, 0.0)))
    bound_ref[...] = jnp.broadcast_to(high, bound_ref.shape)


def solve_kernel(bounds_ref, wide_ref, centre_ref, height_ref):
    rows, cols = height_ref.shape
    tall, wide = centre_ref.shape
    top = 2.0 * jnp.max(bounds_ref[...], axis=0, keepdims=True) - surface_term
    top = jnp.concatenate([top] * (wide // 128), axis=1)
    theta = 0.5 * (top + surface_term)
    delta = 0.5 * (top - surface_term)
    sigma = theta / delta
    wet_depth, ocean, centre = wide_ref[1], wide_ref[2], centre_ref[...]
    residual = wide_ref[0]
    direction = residual / theta
    total = direction
    recur = 1.0 / sigma
    for step in range(ITERS):
        image = centre * direction - 0.5 * (
            wet_depth * around(ocean * direction) + ocean * around(wet_depth * direction)
        )
        residual = residual - image
        recur_next = 1.0 / (2.0 * sigma - recur)
        direction = (recur_next * recur) * direction + (2.0 * recur_next / delta) * residual
        recur = recur_next
        total = total + direction
    height_ref[...] = total[HALO : HALO + rows, :cols]


def call(kernel, outs, *args, scratch=()):
    return pl.pallas_call(
        kernel,
        in_specs=[SMEM if arg.ndim == 1 else VMEM for arg in args],
        out_specs=[VMEM] * len(outs),
        out_shape=[jax.ShapeDtypeStruct(shape, jnp.float32) for shape in outs],
        scratch_shapes=[pltpu.VMEM(shape, jnp.float32) for shape in scratch],
        compiler_params=pltpu.CompilerParams(vmem_limit_bytes=4 * 2**20),
        name=kernel.__name__,
    )(*args)


def local(heat, conduct, spacing, wet, water, depth):
    rows, cols = depth.shape
    tall, wide = rows + 2 * HALO, cols + 128
    ring = lax.axis_size(COL)
    index = lax.axis_index(COL).astype(jnp.int32).reshape(1)
    diffused, forcing, to_north, to_south = mix(heat, conduct, spacing, wet, water, depth)
    down = [(i, i + 1) for i in range(lax.axis_size(ROW) - 1)]
    north = lax.ppermute(to_south, ROW, down)
    south = lax.ppermute(to_north, ROW, [(b, a) for a, b in down])
    fields, slots = call(
        edge_kernel, [(3, tall, cols), (ring * 8, 128)], forcing, depth, water, north, south, scratch=[(128, 128)]
    )
    slots = lax.all_to_all(slots, COL, 0, 0, tiled=True)
    full, centre, bound = call(
        weights_kernel,
        [(3, tall, wide), (tall, wide), (lax.axis_size(ROW), 128)],
        index, slots, fields, scratch=[(128, 128)],
    )
    bounds = lax.all_to_all(bound, ROW, 0, 0, tiled=True)
    (height,) = call(solve_kernel, [(rows, cols)], bounds, full, centre)
    return diffused, height


def solution(mesh):
    torus = Mesh(mesh.devices.reshape(16, 4, 8, 2), ROW + COL)
    return jax.shard_map(
        local,
        mesh=torus,
        in_specs=(P(None, ROW, COL), P(None, ROW, COL), P(), P(ROW, COL), P(ROW, COL), P(ROW, COL)),
        out_specs=(P(None, ROW, COL), P(ROW, COL)),
        check_vma=False,
    )
```

time: 103 us -> 72.8 us (0.71)
  blocking collectives: 65.3 us -> 31.5 us
  waiting for transfers between devices: 4.98 us -> 11.2 us
  Pallas kernels: 12.3 us -> 7.15 us
  starting transfers between devices: 17.8 us -> 21.1 us
    all_to_all x1, blocking collectives: 65.3 us -> 31.5 us  [local(): bounds = lax.all_to_all(bound, ROW, 0, 0, tiled=True)]
    all_to_all x0 -> x1, starting transfers between devices: none -> 15.9 us  [local(): slots = lax.all_to_all(slots, COL, 0, 0, tiled=True)]
    ppermute x2 -> x0, starting transfers between devices: 12.6 us -> none  [the longest x1 12.6 us: local(): east = lax.ppermute(edge, COL, [(b, a) for a, b in ring])]
    all_to_all x0 -> x1, waiting for transfers between devices: none -> 7.82 us  [local(): slots = lax.all_to_all(slots, COL, 0, 0, tiled=True)]
    pallas_call x4 -> x3, Pallas kernels: 7.36 us -> 2.55 us  [call(): pl.pallas_call(kernel, in_specs=[SMEM if arg.ndim == 1 else VMEM for arg...]
    ppermute x2 -> x0, waiting for transfers between devices: 1.61 us -> none  [the longest x1 1.1 us: local(): east = lax.ppermute(edge, COL, [(b, a) for a, b in ring])]
  transfers between devices with their start and end apart: 4 -> 3, of which waited for: 3 -> 2; matrix products, arithmetic and copies ran while one was open for 0% -> 0% of each run, Pallas kernels for 0% -> 0%
where the time goes in v1:
time: 72.8 us; the launch traced here: 72.4 us
  blocking collectives  31.5 us (43%)
  starting transfers between devices  21.1 us (29%)
  waiting for transfers between devices  11.2 us (15%)
  Pallas kernels  7.15 us (10%)
  local copies, waits for them, and re-layouts  0.77 us (1%)
    all_to_all x1, blocking collectives, local(): bounds = lax.all_to_all(bound, ROW, 0, 0, tiled=True)  31.5 us
    all_to_all x1, starting transfers between devices, local(): slots = lax.all_to_all(slots, COL, 0, 0, tiled=True)  15.9 us
    all_to_all x1, waiting for transfers between devices, local(): slots = lax.all_to_all(slots, COL, 0, 0, tiled=True)  7.82 us
    pallas_call x1, Pallas kernels, mix(): pl.pallas_call(mix_kernel, in_specs=[pl.BlockSpec(memory_space=pltpu.SMEM...  4.61 us
    ppermute x1, starting transfers between devices, local(): north = lax.ppermute(to_south, ROW, down)  3.93 us
    ppermute x1, waiting for transfers between devices, local(): south = lax.ppermute(to_north, ROW, [(b, a) for a, b in down])  3.38 us
    pallas_call x3, Pallas kernels, call(): pl.pallas_call(kernel, in_specs=[SMEM if arg.ndim == 1 else VMEM for arg...  2.55 us
  transfers between devices with their start and end apart: 3, of which 2 were waited for; matrix products, arithmetic and copies ran while one was open for 0% of the time, Pallas kernels for 0%

profile of v1, /device:TPU:1, one launch (start us, length us, event | category | flops | bytes accessed | tf_op | source)
XLA Modules:
  0.0 72.4 jit_solution(517007234975795411)
XLA Ops:
  0.6 0.0 copy-start.1
  0.6 0.0 copy-start
  0.7 4.6 %mix.1 = (f32[48,32,256]{2,1,0:T(8,128)}, f32[32,256]{1,0:T(8,128)}, f32[12,256]{1,0:T(8,128)}, f32[12,256]{1,0:T(8,128)}) custom-call(f32[48]{0:T(128)} %spacing_ref.1, s32[32,256]{1,0:T(8,128)} %wet_hbm.1, s32[32,256]{1,0:T(8,128)} %water_ref.1, f32[32,256]{1,0:T(8,128)} %depth_ref.1, bf16[48,32,256]{2,1,0:T(8,128)(2,1)} %heat_hbm.1, ...), custom_call_target="tpu_custom_call" | custom-call | tf_op jit(solution)/shard_map/mix/pallas_call | solution.py:128
  5.3 3.9 %collective-permute-start = (f32[12,256]{1,0:T(8,128)}, f32[12,256]{1,0:T(8,128)S(1)}, u32[]{:S(2)}, u32[]{:S(2)}) collective-permute-start(f32[12,256]{1,0:T(8,128)} %get-tuple-element.13), channel_id=1, source_target_pairs={{0,16},{16,32},{32,48},{48,64},{64,80},{80,96},{96,112},{112,128},... | collective-permute-start | bytes 36872 | tf_op jit(solution)/shard_map/ppermute | solution.py:272
  9.2 1.3 %collective-permute-start.1 = (f32[12,256]{1,0:T(8,128)}, f32[12,256]{1,0:T(8,128)S(1)}, u32[]{:S(2)}, u32[]{:S(2)}) collective-permute-start(f32[12,256]{1,0:T(8,128)} %get-tuple-element.14), channel_id=1, source_target_pairs={{16,0},{32,16},{48,32},{64,48},{80,64},{96,80},{112,96},{128,112},... | collective-permute-start | bytes 36872 | tf_op jit(solution)/shard_map/ppermute | solution.py:273
  10.5 0.0 collective-permute-done.north_ref
  10.5 3.4 %collective-permute-done.1.south_ref = f32[12,256]{1,0:T(8,128)S(1)} collective-permute-done((f32[12,256]{1,0:T(8,128)}, f32[12,256]{1,0:T(8,128)S(1)}, u32[]{:S(2)}, u32[]{:S(2)}) %collective-permute-start.1) | collective-permute-done | bytes 12320 | tf_op jit(solution)/shard_map/ppermute | solution.py:273
  13.9 0.0 copy-done.1
  13.9 0.0 copy-done
  13.9 0.0 copy-start.2
  13.9 0.8 %copy-done.2 = f32[32,256]{1,0:T(8,128)S(1)} copy-done((f32[32,256]{1,0:T(8,128)S(1)}, f32[32,256]{1,0:T(8,128)}, u32[]{:S(2)}) %copy-start.2) | copy-done | bytes 32792
  14.7 0.9 %edge_kernel.1 = (f32[3,40,256]{2,1,0:T(8,128)S(1)}, f32[128,128]{1,0:T(8,128)}) custom-call(f32[32,256]{1,0:T(8,128)S(1)} %copy-done.2, f32[32,256]{1,0:T(8,128)S(1)} %copy-done.1, s32[32,256]{1,0:T(8,128)S(1)} %copy-done, f32[12,256]{1,0:T(8,128)S(1)} %collective-permute-done.north_ref, f32[12,256]{1,0:T(8,128)S(1)} %collective-permute-done.1.south_ref), custom_call_target="tpu_custom_call" | custom-call | tf_op jit(solution)/shard_map/edge_kernel/pallas_call | solution.py:254
  15.6 15.9 %all-to-all-start = ((f32[16,8,128]{2,1,0:T(8,128)}), f32[16,8,128]{2,1,0:T(8,128)S(1)}, u32[]{:S(2)}, u32[]{:S(2)}) async-start(f32[16,8,128]{2,1,0:T(8,128)} %bitcast.1), calls=%async_computation | async-start | bytes 131072 | tf_op jit(solution)/shard_map/all_to_all | solution.py:277
  31.5 7.8 %all-to-all-done = f32[16,8,128]{2,1,0:T(8,128)S(1)} async-done(((f32[16,8,128]{2,1,0:T(8,128)}), f32[16,8,128]{2,1,0:T(8,128)S(1)}, u32[]{:S(2)}, u32[]{:S(2)}) %all-to-all-start) | async-done | bytes 65568 | tf_op jit(solution)/shard_map/all_to_all | solution.py:277
  39.3 0.4 weights_kernel.1
  39.7 31.5 %all_to_all.22 = f32[64,1,128]{2,1,0:T(1,128)S(1)} all-to-all(f32[64,1,128]{2,1,0:T(1,128)S(1)} %bitcast.9), channel_id=1, replica_groups=mesh['row_0'=16,'row_1'=4,'col_0'=8,'col_1'=2] {'row_0','row_1'}, dimensions={0} | all-to-all | bytes 65536 | tf_op jit(solution)/shard_map/all_to_all | solution.py:283
  71.1 1.2 %solve_kernel.1 = f32[32,256]{1,0:T(8,128)} custom-call(f32[64,128]{1,0:T(8,128)S(1)} %bitcast.8, f32[3,40,384]{2,1,0:T(8,128)S(1)} %get-tuple-element.18.wide_ref, f32[40,384]{1,0:T(8,128)S(1)} %get-tuple-element.19.centre_ref), custom_call_target="tpu_custom_call" | custom-call | tf_op jit(solution)/shard_map/solve_kernel/pallas_call | solution.py:254
Async XLA Ops:
  0.6 13.3 %copy-start.1 = (f32[32,256]{1,0:T(8,128)S(1)}, f32[32,256]{1,0:T(8,128)}, u32[]{:S(2)}) copy-start(f32[32,256]{1,0:T(8,128)} %depth_ref.1) | copy-start | bytes 98308
  0.6 13.3 %copy-start = (s32[32,256]{1,0:T(8,128)S(1)}, s32[32,256]{1,0:T(8,128)}, u32[]{:S(2)}) copy-start(s32[32,256]{1,0:T(8,128)} %water_ref.1) | copy-start | bytes 98308
  5.3 5.2 %collective-permute-start = (f32[12,256]{1,0:T(8,128)}, f32[12,256]{1,0:T(8,128)S(1)}, u32[]{:S(2)}, u32[]{:S(2)}) collective-permute-start(f32[12,256]{1,0:T(8,128)} %get-tuple-element.13), channel_id=1, source_target_pairs={{0,16},{16,32},{32,48},{48,64},{64,80},{80,96},{96,112},{112,128},... | collective-permute-start | bytes 36872 | tf_op jit(solution)/shard_map/ppermute | solution.py:272
  9.2 4.7 %collective-permute-start.1 = (f32[12,256]{1,0:T(8,128)}, f32[12,256]{1,0:T(8,128)S(1)}, u32[]{:S(2)}, u32[]{:S(2)}) collective-permute-start(f32[12,256]{1,0:T(8,128)} %get-tuple-element.14), channel_id=1, source_target_pairs={{16,0},{32,16},{48,32},{64,48},{80,64},{96,80},{112,96},{128,112},... | collective-permute-start | bytes 36872 | tf_op jit(solution)/shard_map/ppermute | solution.py:273
  13.9 0.8 %copy-start.2 = (f32[32,256]{1,0:T(8,128)S(1)}, f32[32,256]{1,0:T(8,128)}, u32[]{:S(2)}) copy-start(f32[32,256]{1,0:T(8,128)} %get-tuple-element.12.forcing_ref) | copy-start | bytes 98308
  15.6 23.7 %all-to-all-start = ((f32[16,8,128]{2,1,0:T(8,128)}), f32[16,8,128]{2,1,0:T(8,128)S(1)}, u32[]{:S(2)}, u32[]{:S(2)}) async-start(f32[16,8,128]{2,1,0:T(8,128)} %bitcast.1), calls=%async_computation | async-start | bytes 131072 | tf_op jit(solution)/shard_map/all_to_all | solution.py:277

commit v2 on v1

v2 whole, which is shorter than its diff:
```python
import functools
import math

import jax
import jax.numpy as jnp
from jax import lax
from jax.experimental import pallas as pl
from jax.experimental.pallas import tpu as pltpu
from jax.sharding import Mesh
from jax.sharding import PartitionSpec as P


ITERS = 4
CHUNK = 6
ROW = ("row_0", "row_1")
COL = ("col_0", "col_1")
HALO = ITERS
VMEM = pl.BlockSpec(memory_space=pltpu.VMEM)
SMEM = pl.BlockSpec(memory_space=pltpu.SMEM)
surface_term = 0.5


def mix_kernel(
    spacing_ref, wet_hbm, water_hbm, heat_hbm, conduct_hbm,
    out_hbm, forcing_hbm, north_hbm, south_hbm,
    forcing_ref, north_ref, south_ref, wet_ref, water_ref, heat_buf, conduct_buf, ratio_buf, value_buf,
    plane_sem, edge_sem, heat_sem, conduct_sem, out_sem,
):
    levels, rows, cols = heat_buf.shape
    chunks = levels // CHUNK
    planes = [
        pltpu.make_async_copy(source, target, plane_sem.at[slot])
        for slot, (source, target) in enumerate(((wet_hbm, wet_ref), (water_hbm, water_ref)))
    ]
    planes[0].start()

    def fetch(chunk):
        first = chunk * CHUNK
        count = min(CHUNK, levels - 1 - first)
        return (
            pltpu.make_async_copy(
                heat_hbm.at[pl.ds(first, CHUNK)], heat_buf.at[pl.ds(first, CHUNK)], heat_sem.at[chunk]
            ),
            pltpu.make_async_copy(
                conduct_hbm.at[pl.ds(first, count)], conduct_buf.at[pl.ds(first, count)], conduct_sem.at[chunk]
            ),
        )

    def flush(chunk):
        first = chunk * CHUNK
        return pltpu.make_async_copy(
            value_buf.at[pl.ds(first, CHUNK)], out_hbm.at[pl.ds(first, CHUNK)], out_sem.at[chunk]
        )

    for chunk in range(chunks):
        for copy in fetch(chunk):
            copy.start()
    planes[1].start()
    planes[0].wait()
    wet = wet_ref[...]
    zero = jnp.zeros((rows, cols), jnp.float32)

    def down(level, carry, last=False):
        couple_prev, ratio_prev, value_prev = carry
        spacing = spacing_ref[level]
        if last:
            couple = zero
        else:
            couple = jnp.where(level + 1 < wet, conduct_buf[level].astype(jnp.float32), 0.0)
        source = spacing * heat_buf[level].astype(jnp.float32)
        pivot = spacing + couple_prev + couple - couple_prev * ratio_prev
        inverse = 1.0 / pivot
        ratio = couple * inverse
        value = (source + couple_prev * value_prev) * inverse
        ratio_buf[level] = ratio
        value_buf[level] = value
        return couple, ratio, value

    carry = (zero, zero, zero)
    for chunk in range(chunks):
        for copy in fetch(chunk):
            copy.wait()
        first = chunk * CHUNK
        stop = min(first + CHUNK, levels - 1)
        carry = lax.fori_loop(first, stop, down, carry)
    carry = down(levels - 1, carry, last=True)

    def up(step, carry, first):
        below, total = carry
        level = first + CHUNK - 1 - step
        result = value_buf[level] + ratio_buf[level] * below
        value_buf[level] = result
        total = total + jnp.where(level < wet, spacing_ref[level] * result, 0.0)
        return result, total

    carry = (zero, zero)
    for chunk in reversed(range(chunks)):
        carry = lax.fori_loop(0, CHUNK, functools.partial(up, first=chunk * CHUNK), carry)
        flush(chunk).start()
    planes[1].wait()
    forcing = water_ref[...].astype(jnp.float32) * carry[1] * (1.0 / math.sqrt(levels))
    forcing_ref[...] = forcing
    north_ref[...] = forcing[:HALO]
    south_ref[...] = forcing[rows - HALO :]
    edges = [
        pltpu.make_async_copy(source, target, edge_sem.at[slot])
        for slot, (source, target) in enumerate(
            ((north_ref, north_hbm), (south_ref, south_hbm), (forcing_ref, forcing_hbm))
        )
    ]
    for copy in edges:
        copy.start()
    for chunk in reversed(range(chunks)):
        flush(chunk).wait()
    for copy in edges:
        copy.wait()


def mix(heat, conduct, spacing, wet, water):
    levels, rows, cols = heat.shape
    chunks = levels // CHUNK
    hbm = pl.BlockSpec(memory_space=pltpu.HBM)
    return pl.pallas_call(
        mix_kernel,
        in_specs=[SMEM, hbm, hbm, hbm, hbm],
        out_specs=[hbm, hbm, hbm, hbm],
        out_shape=[
            jax.ShapeDtypeStruct((levels, rows, cols), jnp.float32),
            jax.ShapeDtypeStruct((rows, cols), jnp.float32),
            jax.ShapeDtypeStruct((HALO, cols), jnp.float32),
            jax.ShapeDtypeStruct((HALO, cols), jnp.float32),
        ],
        scratch_shapes=[
            pltpu.VMEM((rows, cols), jnp.float32),
            pltpu.VMEM((HALO, cols), jnp.float32),
            pltpu.VMEM((HALO, cols), jnp.float32),
            pltpu.VMEM((rows, cols), wet.dtype),
            pltpu.VMEM((rows, cols), water.dtype),
            pltpu.VMEM((levels, rows, cols), heat.dtype),
            pltpu.VMEM((levels, rows, cols), conduct.dtype),
            pltpu.VMEM((levels, rows, cols), jnp.float32),
            pltpu.VMEM((levels, rows, cols), jnp.float32),
            pltpu.SemaphoreType.DMA((2,)),
            pltpu.SemaphoreType.DMA((3,)),
            pltpu.SemaphoreType.DMA((chunks,)),
            pltpu.SemaphoreType.DMA((chunks,)),
            pltpu.SemaphoreType.DMA((chunks,)),
        ],
        name="mix",
    )(spacing, wet, water, heat, conduct)


def around(field):
    tall, wide = field.shape
    beside = pltpu.roll(field, 1, 0) + pltpu.roll(field, tall - 1, 0)
    slant = field + 0.5 * beside
    return beside + (pltpu.roll(slant, 1, 1) + pltpu.roll(slant, wide - 1, 1))


def centre_of(wet_depth, ocean):
    return surface_term + 0.5 * (wet_depth * around(ocean) + ocean * around(wet_depth))


def most(field):
    return jnp.max(jnp.max(field, axis=0, keepdims=True), axis=1, keepdims=True)


def rows_kernel(depth_ref, water_ref, north_ref, south_ref):
    rows = depth_ref.shape[0]
    for slot, field in enumerate((depth_ref[...], water_ref[...].astype(jnp.float32))):
        north_ref[slot * HALO : (slot + 1) * HALO] = field[:HALO]
        south_ref[slot * HALO : (slot + 1) * HALO] = field[rows - HALO :]


def edge_kernel(depth_ref, water_ref, north_ref, south_ref, tall_ref, slots_ref, pack_ref):
    rows, cols = depth_ref.shape
    tall = rows + 2 * HALO
    lane = lax.broadcasted_iota(jnp.int32, (tall, 128), 1)
    for slot, field in enumerate((depth_ref[...], water_ref[...].astype(jnp.float32))):
        tall_ref[slot, :HALO] = north_ref[slot * HALO : (slot + 1) * HALO]
        tall_ref[slot, HALO : HALO + rows] = field
        tall_ref[slot, HALO + rows :] = south_ref[slot * HALO : (slot + 1) * HALO]
        pack_ref[slot * tall : (slot + 1) * tall] = jnp.where(
            lane < 64, tall_ref[slot, :, :128], tall_ref[slot, :, cols - 128 :]
        )
    ocean = tall_ref[1]
    centre = centre_of(tall_ref[0] * ocean, ocean)
    row = lax.broadcasted_iota(jnp.int32, (tall, cols), 0)
    col = lax.broadcasted_iota(jnp.int32, (tall, cols), 1)
    inner = (row >= HALO) & (row < HALO + rows) & (col >= 1) & (col < cols - 1)
    pack_ref[2 * tall :] = jnp.broadcast_to(most(jnp.where(inner, centre, 0.0)), (128 - 2 * tall, 128))
    turned = pack_ref[...].T
    which = lax.broadcasted_iota(jnp.int32, (8, 128), 0)
    tile = jnp.where(which < HALO, turned[:8], turned[120:])
    for slot in range(slots_ref.shape[0] // 8):
        slots_ref[slot * 8 : (slot + 1) * 8] = tile


def forcing_kernel(forcing_ref, north_ref, south_ref, tall_ref, edge_ref):
    rows, cols = forcing_ref.shape
    tall_ref[:HALO] = north_ref[...]
    tall_ref[HALO : HALO + rows] = forcing_ref[...]
    tall_ref[HALO + rows :] = south_ref[...]
    lane = lax.broadcasted_iota(jnp.int32, edge_ref.shape, 1)
    edge_ref[...] = jnp.where(lane < 64, tall_ref[:, :128], tall_ref[:, cols - 128 :])


def weights_kernel(index_ref, slots_ref, tall_ref, wide_ref, bound_ref, pack_ref):
    tall, _ = tall_ref.shape[1:]
    devices = slots_ref.shape[0] // 8
    index = index_ref[0]
    which = lax.broadcasted_iota(jnp.int32, (8, 128), 0)
    east = slots_ref[pl.ds(pl.multiple_of(lax.rem(index + 1, devices) * 8, 8), 8)]
    west = slots_ref[pl.ds(pl.multiple_of(lax.rem(index + devices - 1, devices) * 8, 8), 8)]
    slots = slots_ref[...]
    joint = pltpu.roll(slots, HALO, 0)
    joint_ocean = pltpu.roll(joint, 128 - tall, 1)
    joint_centre = centre_of(joint * joint_ocean, joint_ocean)
    row = lax.broadcasted_iota(jnp.int32, joint.shape, 0) % 8
    lane = lax.broadcasted_iota(jnp.int32, joint.shape, 1)
    seam = ((row == HALO - 1) | (row == HALO)) & (lane >= HALO) & (lane < tall - HALO)
    high = most(jnp.where(seam, joint_centre, jnp.where(lane >= 2 * tall, slots, 0.0)))
    bound_ref[...] = jnp.broadcast_to(high, bound_ref.shape)
    pack_ref[...] = jnp.zeros((128, 128), jnp.float32)
    pack_ref[:8] = jnp.where(which < HALO, east, 0.0)
    pack_ref[120:] = jnp.where(which >= HALO, west, 0.0)
    turned = pack_ref[...].T
    depth, ocean = (
        jnp.concatenate([tall_ref[slot], turned[slot * tall : (slot + 1) * tall]], axis=1) for slot in range(2)
    )
    wet_depth = depth * ocean
    wide_ref[0] = wet_depth
    wide_ref[1] = ocean
    wide_ref[2] = centre_of(wet_depth, ocean)


def solve_kernel(bounds_ref, wide_ref, tall_ref, west_ref, east_ref, height_ref):
    rows, cols = height_ref.shape
    tall, wide = wide_ref.shape[1:]
    top = 2.0 * jnp.max(bounds_ref[...], axis=0, keepdims=True) - surface_term
    top = jnp.concatenate([top] * (wide // 128), axis=1)
    theta = 0.5 * (top + surface_term)
    delta = 0.5 * (top - surface_term)
    sigma = theta / delta
    wet_depth, ocean, centre = wide_ref[0], wide_ref[1], wide_ref[2]
    lane = lax.broadcasted_iota(jnp.int32, (tall, 128), 1)
    side = jnp.where(lane < HALO, east_ref[...], jnp.where(lane >= 128 - HALO, west_ref[...], 0.0))
    residual = jnp.concatenate([tall_ref[...], side], axis=1)
    direction = residual / theta
    total = direction
    recur = 1.0 / sigma
    for _ in range(ITERS):
        image = centre * direction - 0.5 * (
            wet_depth * around(ocean * direction) + ocean * around(wet_depth * direction)
        )
        residual = residual - image
        recur_next = 1.0 / (2.0 * sigma - recur)
        direction = (recur_next * recur) * direction + (2.0 * recur_next / delta) * residual
        recur = recur_next
        total = total + direction
    height_ref[...] = total[HALO : HALO + rows, :cols]


def call(kernel, outs, *args, scratch=(), limit=4 * 2**20):
    return pl.pallas_call(
        kernel,
        in_specs=[SMEM if arg.ndim == 1 else VMEM for arg in args],
        out_specs=[VMEM] * len(outs),
        out_shape=[jax.ShapeDtypeStruct(shape, jnp.float32) for shape in outs],
        scratch_shapes=[pltpu.VMEM(shape, jnp.float32) for shape in scratch],
        compiler_params=pltpu.CompilerParams(vmem_limit_bytes=limit),
    )(*args)


def step(heat, conduct, spacing, wet, water, depth):
    rows, cols = depth.shape
    tall, wide = rows + 2 * HALO, cols + 128
    ring = lax.axis_size(COL)
    index = lax.axis_index(COL).astype(jnp.int32).reshape(1)
    down = [(i, i + 1) for i in range(lax.axis_size(ROW) - 1)]
    right = [(i, (i + 1) % ring) for i in range(ring)]
    up, left = ([(b, a) for a, b in pairs] for pairs in (down, right))

    to_north, to_south = call(rows_kernel, [(2 * HALO, cols)] * 2, depth, water)
    north = lax.ppermute(to_south, ROW, down)
    south = lax.ppermute(to_north, ROW, up)
    diffused, forcing, forcing_north, forcing_south = mix(heat, conduct, spacing, wet, water)
    fields, slots = call(
        edge_kernel, [(2, tall, cols), (ring * 8, 128)], depth, water, north, south, scratch=[(128, 128)]
    )
    from_north = lax.ppermute(forcing_south, ROW, down)
    from_south = lax.ppermute(forcing_north, ROW, up)
    slots = lax.all_to_all(slots, COL, 0, 0, tiled=True)
    forcing, edge = call(forcing_kernel, [(tall, cols), (tall, 128)], forcing, from_north, from_south)
    full, bound = call(
        weights_kernel, [(3, tall, wide), (lax.axis_size(ROW), 128)], index, slots, fields, scratch=[(128, 128)]
    )
    west = lax.ppermute(edge, COL, right)
    east = lax.ppermute(edge, COL, left)
    bounds = lax.all_to_all(bound, ROW, 0, 0, tiled=True)
    (height,) = call(solve_kernel, [(rows, cols)], bounds, full, forcing, west, east)
    return diffused, height


def solution(mesh):
    torus = Mesh(mesh.devices.reshape(16, 4, 8, 2), ROW + COL)
    return jax.shard_map(
        step,
        mesh=torus,
        in_specs=(P(None, ROW, COL), P(None, ROW, COL), P(), P(ROW, COL), P(ROW, COL), P(ROW, COL)),
        out_specs=(P(None, ROW, COL), P(ROW, COL)),
        check_vma=False,
    )
```

time: 72.8 us -> 76 us (1.044)
  the two profiles are of different devices: /device:TPU:1 before, /device:TPU:6 now
where the time goes in v2:
time: 76 us; the launch traced here: 75.4 us
  starting transfers between devices  42 us (55%)
  waiting for transfers between devices  22.8 us (30%)
  Pallas kernels  7.7 us (10%)
  local copies, waits for them, and re-layouts  2.27 us (3%)
    all_to_all x1, starting transfers between devices, step(): bounds = lax.all_to_all(bound, ROW, 0, 0, tiled=True)  22.3 us
    all_to_all x1, waiting for transfers between devices, step(): slots = lax.all_to_all(slots, COL, 0, 0, tiled=True)  7.79 us
    all_to_all x1, starting transfers between devices, step(): slots = lax.all_to_all(slots, COL, 0, 0, tiled=True)  7.21 us
    ppermute x1, waiting for transfers between devices, step(): south = lax.ppermute(to_north, ROW, up)  5.72 us
    ppermute x1, waiting for transfers between devices, step(): from_south = lax.ppermute(forcing_north, ROW, up)  5.33 us
    pallas_call x1, Pallas kernels, mix(): pl.pallas_call(mix_kernel, in_specs=[SMEM, hbm, hbm, hbm, hbm], out_specs...  4.53 us
    ppermute x1, starting transfers between devices, step(): north = lax.ppermute(to_south, ROW, down)  4.18 us
    ppermute x1, starting transfers between devices, step(): from_north = lax.ppermute(forcing_south, ROW, down)  3.37 us
  transfers between devices with their start and end apart: 8, of which 5 were waited for; matrix products, arithmetic and copies ran while one was open for 0% of the time, Pallas kernels for 6%

profile of v2, /device:TPU:6, one launch (start us, length us, event | category | flops | bytes accessed | tf_op | source)
XLA Modules:
  0.0 75.4 jit_solution(10230461673383855996)
XLA Ops:
  0.6 0.0 copy-start
  0.6 0.7 copy-done
  1.4 0.8 %copy-done.1 = f32[32,256]{1,0:T(8,128)S(1)} copy-done((f32[32,256]{1,0:T(8,128)S(1)}, f32[32,256]{1,0:T(8,128)}, u32[]{:S(2)}) %copy-start.1) | copy-done | bytes 32792
  2.2 4.2 %collective-permute-start = (f32[8,256]{1,0:T(8,128)S(1)}, f32[8,256]{1,0:T(8,128)S(1)}, u32[]{:S(2)}, u32[]{:S(2)}) collective-permute-start(f32[8,256]{1,0:T(8,128)S(1)} %get-tuple-element.15), channel_id=1, source_target_pairs={{0,16},{16,32},{32,48},{48,64},{64,80},{80,96},{96,112},{112,128},... | collective-permute-start | bytes 24584 | tf_op jit(solution)/shard_map/ppermute | solution.py:285
  6.3 1.9 %collective-permute-start.1 = (f32[8,256]{1,0:T(8,128)S(1)}, f32[8,256]{1,0:T(8,128)S(1)}, u32[]{:S(2)}, u32[]{:S(2)}) collective-permute-start(f32[8,256]{1,0:T(8,128)S(1)} %get-tuple-element.16), channel_id=1, source_target_pairs={{16,0},{32,16},{48,32},{64,48},{80,64},{96,80},{112,96},{128,112},... | collective-permute-start | bytes 24584 | tf_op jit(solution)/shard_map/ppermute | solution.py:286
  8.3 0.0 collective-permute-done.north_ref
  8.3 5.7 %collective-permute-done.1.south_ref = f32[8,256]{1,0:T(8,128)S(1)} collective-permute-done((f32[8,256]{1,0:T(8,128)S(1)}, f32[8,256]{1,0:T(8,128)S(1)}, u32[]{:S(2)}, u32[]{:S(2)}) %collective-permute-start.1) | collective-permute-done | bytes 8224 | tf_op jit(solution)/shard_map/ppermute | solution.py:286
  14.0 0.9 %shard_map.78 = (f32[2,40,256]{2,1,0:T(8,128)S(1)}, f32[128,128]{1,0:T(8,128)}) custom-call(f32[32,256]{1,0:T(8,128)S(1)} %copy-done.1, s32[32,256]{1,0:T(8,128)S(1)} %copy-done, f32[8,256]{1,0:T(8,128)S(1)} %collective-permute-done.north_ref, f32[8,256]{1,0:T(8,128)S(1)} %collective-permute-done.1.south_ref), custom_call_target="tpu_custom_call" | custom-call | tf_op jit(solution)/shard_map/pallas_call | solution.py:265
  14.9 7.2 %all-to-all-start = ((f32[16,8,128]{2,1,0:T(8,128)}), f32[16,8,128]{2,1,0:T(8,128)S(1)}, u32[]{:S(2)}, u32[]{:S(2)}) async-start(f32[16,8,128]{2,1,0:T(8,128)} %bitcast.1), calls=%async_computation | async-start | bytes 131072 | tf_op jit(solution)/shard_map/all_to_all | solution.py:293
  22.1 7.8 %all-to-all-done = f32[16,8,128]{2,1,0:T(8,128)S(1)} async-done(((f32[16,8,128]{2,1,0:T(8,128)}), f32[16,8,128]{2,1,0:T(8,128)S(1)}, u32[]{:S(2)}, u32[]{:S(2)}) %all-to-all-start) | async-done | bytes 65568 | tf_op jit(solution)/shard_map/all_to_all | solution.py:293
  29.9 1.0 %shard_map.79 = (f32[3,40,384]{2,1,0:T(8,128)S(1)}, f32[64,128]{1,0:T(8,128)}) custom-call(s32[1]{0:T(128)} %bitcast.index_ref, f32[128,128]{1,0:T(8,128)S(1)} %bitcast.7, f32[2,40,256]{2,1,0:T(8,128)S(1)} %get-tuple-element.18.tall_ref), custom_call_target="tpu_custom_call" | custom-call | tf_op jit(solution)/shard_map/pallas_call | solution.py:265
  30.9 22.3 %all-to-all-start.1 = ((f32[64,1,128]{2,1,0:T(1,128)}), f32[64,1,128]{2,1,0:T(1,128)S(1)}, u32[]{:S(2)}, u32[]{:S(2)}) async-start(f32[64,1,128]{2,1,0:T(1,128)} %bitcast.4), calls=%async_computation.1 | async-start | bytes 65536 | tf_op jit(solution)/shard_map/all_to_all | solution.py:300
  53.2 4.5 %mix.1 = (f32[48,32,256]{2,1,0:T(8,128)}, f32[32,256]{1,0:T(8,128)}, f32[4,256]{1,0:T(4,128)}, f32[4,256]{1,0:T(4,128)}) custom-call(f32[48]{0:T(128)} %spacing_ref.1, s32[32,256]{1,0:T(8,128)} %wet_hbm.1, s32[32,256]{1,0:T(8,128)} %water_ref.3, bf16[48,32,256]{2,1,0:T(8,128)(2,1)} %heat_hbm.1, bf16[47,32,256]{2,1,0:T(8,128)(2,1)} %conduct_hbm.1), custom_call_target="tpu_custom_call" | custom-call | tf_op jit(solution)/shard_map/mix/pallas_call | solution.py:123
  57.8 3.4 %collective-permute-start.2 = (f32[4,256]{1,0:T(4,128)}, f32[4,256]{1,0:T(4,128)S(1)}, u32[]{:S(2)}, u32[]{:S(2)}) collective-permute-start(f32[4,256]{1,0:T(4,128)} %get-tuple-element.22), channel_id=1, source_target_pairs={{0,16},{16,32},{32,48},{48,64},{64,80},{80,96},{96,112},{112,128},... | collective-permute-start | bytes 12296 | tf_op jit(solution)/shard_map/ppermute | solution.py:291
  61.1 2.5 %collective-permute-start.3 = (f32[4,256]{1,0:T(4,128)}, f32[4,256]{1,0:T(4,128)S(1)}, u32[]{:S(2)}, u32[]{:S(2)}) collective-permute-start(f32[4,256]{1,0:T(4,128)} %get-tuple-element.23), channel_id=1, source_target_pairs={{16,0},{32,16},{48,32},{64,48},{80,64},{96,80},{112,96},{128,112},... | collective-permute-start | bytes 12296 | tf_op jit(solution)/shard_map/ppermute | solution.py:292
  63.6 0.0 collective-permute-done.2.north_ref
  63.6 5.3 %collective-permute-done.3.south_ref = f32[4,256]{1,0:T(4,128)S(1)} collective-permute-done((f32[4,256]{1,0:T(4,128)}, f32[4,256]{1,0:T(4,128)S(1)}, u32[]{:S(2)}, u32[]{:S(2)}) %collective-permute-start.3) | collective-permute-done | bytes 4128 | tf_op jit(solution)/shard_map/ppermute | solution.py:292
  69.0 0.8 %copy-done.2 = f32[32,256]{1,0:T(8,128)S(1)} copy-done((f32[32,256]{1,0:T(8,128)S(1)}, f32[32,256]{1,0:T(8,128)}, u32[]{:S(2)}) %copy-start.2) | copy-done | bytes 32792
  69.7 0.0 collective-permute-start.5
  69.8 0.5 collective-permute-start.4
  70.3 1.0 %collective-permute-done.5.east_ref = f32[40,128]{1,0:T(8,128)S(1)} collective-permute-done((f32[40,128]{1,0:T(8,128)S(1)}, f32[40,128]{1,0:T(8,128)S(1)}, u32[]{:S(2)}, u32[]{:S(2)}) %collective-permute-start.5) | collective-permute-done | bytes 20512 | tf_op jit(solution)/shard_map/ppermute | solution.py:299
  71.2 3.0 %collective-permute-done.4.west_ref = f32[40,128]{1,0:T(8,128)S(1)} collective-permute-done((f32[40,128]{1,0:T(8,128)S(1)}, f32[40,128]{1,0:T(8,128)S(1)}, u32[]{:S(2)}, u32[]{:S(2)}) %collective-permute-start.4) | collective-permute-done | bytes 20512 | tf_op jit(solution)/shard_map/ppermute | solution.py:298
  74.2 0.0 all-to-all-done.1
  74.2 1.2 %shard_map.81 = f32[32,256]{1,0:T(8,128)} custom-call(f32[64,128]{1,0:T(8,128)S(1)} %bitcast.8, f32[3,40,384]{2,1,0:T(8,128)S(1)} %get-tuple-element.20.wide_ref, f32[40,256]{1,0:T(8,128)S(1)} %get-tuple-element.24.tall_ref, f32[40,128]{1,0:T(8,128)S(1)} %collective-permute-done.4.west_ref, f32[40,128]{1,0:T(8,128)S(1)} %collective-permute-done.5.east_ref), custom_call_target="tpu_custom_call" | custom-call | tf_op jit(solution)/shard_map/pallas_call | solution.py:265
  (4 shorter events, 0.0 us)
Async XLA Ops:
  0.6 0.8 %copy-start = (s32[32,256]{1,0:T(8,128)S(1)}, s32[32,256]{1,0:T(8,128)}, u32[]{:S(2)}) copy-start(s32[32,256]{1,0:T(8,128)} %water_ref.3) | copy-start | bytes 98308
  1.4 0.8 %copy-start.1 = (f32[32,256]{1,0:T(8,128)S(1)}, f32[32,256]{1,0:T(8,128)}, u32[]{:S(2)}) copy-start(f32[32,256]{1,0:T(8,128)} %depth_ref.3) | copy-start | bytes 98308
  2.2 6.1 %collective-permute-start = (f32[8,256]{1,0:T(8,128)S(1)}, f32[8,256]{1,0:T(8,128)S(1)}, u32[]{:S(2)}, u32[]{:S(2)}) collective-permute-start(f32[8,256]{1,0:T(8,128)S(1)} %get-tuple-element.15), channel_id=1, source_target_pairs={{0,16},{16,32},{32,48},{48,64},{64,80},{80,96},{96,112},{112,128},... | collective-permute-start | bytes 24584 | tf_op jit(solution)/shard_map/ppermute | solution.py:285
  6.3 7.7 %collective-permute-start.1 = (f32[8,256]{1,0:T(8,128)S(1)}, f32[8,256]{1,0:T(8,128)S(1)}, u32[]{:S(2)}, u32[]{:S(2)}) collective-permute-start(f32[8,256]{1,0:T(8,128)S(1)} %get-tuple-element.16), channel_id=1, source_target_pairs={{16,0},{32,16},{48,32},{64,48},{80,64},{96,80},{112,96},{128,112},... | collective-permute-start | bytes 24584 | tf_op jit(solution)/shard_map/ppermute | solution.py:286
  14.9 15.0 %all-to-all-start = ((f32[16,8,128]{2,1,0:T(8,128)}), f32[16,8,128]{2,1,0:T(8,128)S(1)}, u32[]{:S(2)}, u32[]{:S(2)}) async-start(f32[16,8,128]{2,1,0:T(8,128)} %bitcast.1), calls=%async_computation | async-start | bytes 131072 | tf_op jit(solution)/shard_map/all_to_all | solution.py:293
  30.9 43.3 %all-to-all-start.1 = ((f32[64,1,128]{2,1,0:T(1,128)}), f32[64,1,128]{2,1,0:T(1,128)S(1)}, u32[]{:S(2)}, u32[]{:S(2)}) async-start(f32[64,1,128]{2,1,0:T(1,128)} %bitcast.4), calls=%async_computation.1 | async-start | bytes 65536 | tf_op jit(solution)/shard_map/all_to_all | solution.py:300
  57.8 5.9 %collective-permute-start.2 = (f32[4,256]{1,0:T(4,128)}, f32[4,256]{1,0:T(4,128)S(1)}, u32[]{:S(2)}, u32[]{:S(2)}) collective-permute-start(f32[4,256]{1,0:T(4,128)} %get-tuple-element.22), channel_id=1, source_target_pairs={{0,16},{16,32},{32,48},{48,64},{64,80},{80,96},{96,112},{112,128},... | collective-permute-start | bytes 12296 | tf_op jit(solution)/shard_map/ppermute | solution.py:291
  61.1 7.8 %collective-permute-start.3 = (f32[4,256]{1,0:T(4,128)}, f32[4,256]{1,0:T(4,128)S(1)}, u32[]{:S(2)}, u32[]{:S(2)}) collective-permute-start(f32[4,256]{1,0:T(4,128)} %get-tuple-element.23), channel_id=1, source_target_pairs={{16,0},{32,16},{48,32},{64,48},{80,64},{96,80},{112,96},{128,112},... | collective-permute-start | bytes 12296 | tf_op jit(solution)/shard_map/ppermute | solution.py:292
  69.0 0.8 %copy-start.2 = (f32[32,256]{1,0:T(8,128)S(1)}, f32[32,256]{1,0:T(8,128)}, u32[]{:S(2)}) copy-start(f32[32,256]{1,0:T(8,128)} %get-tuple-element.21.forcing_ref) | copy-start | bytes 98308
  69.7 1.5 %collective-permute-start.5 = (f32[40,128]{1,0:T(8,128)S(1)}, f32[40,128]{1,0:T(8,128)S(1)}, u32[]{:S(2)}, u32[]{:S(2)}) collective-permute-start(f32[40,128]{1,0:T(8,128)S(1)} %get-tuple-element.25), channel_id=1, source_target_pairs={{1,0},{2,1},{3,2},{4,3},{5,4},{6,5},{7,6},{8,7},{9,8},{10,9},{11,1... | collective-permute-start | bytes 61448 | tf_op jit(solution)/shard_map/ppermute | solution.py:299
  69.8 4.4 %collective-permute-start.4 = (f32[40,128]{1,0:T(8,128)S(1)}, f32[40,128]{1,0:T(8,128)S(1)}, u32[]{:S(2)}, u32[]{:S(2)}) collective-permute-start(f32[40,128]{1,0:T(8,128)S(1)} %get-tuple-element.25), channel_id=1, source_target_pairs={{0,1},{1,2},{2,3},{3,4},{4,5},{5,6},{6,7},{7,8},{8,9},{9,10},{10,1... | collective-permute-start | bytes 61448 | tf_op jit(solution)/shard_map/ppermute | solution.py:298

commit v3 on v1

--- a/solution.py
+++ b/solution.py
@@ -195,9 +195,11 @@
         slots_ref[slot * 8 : (slot + 1) * 8] = tile
 
 
-def weights_kernel(index_ref, slots_ref, tall_ref, wide_ref, centre_ref, bound_ref, pack_ref):
+def weights_kernel(order, index_ref, sent_ref, tall_ref, wide_ref, centre_ref, bound_ref, pack_ref, slots_ref):
     tall, cols = tall_ref.shape[1:]
-    devices = slots_ref.shape[0] // 8
+    devices = len(order)
+    for slot, device in enumerate(order):
+        slots_ref[device * 8 : (device + 1) * 8] = sent_ref[slot * 8 : (slot + 1) * 8]
     index = index_ref[0]
     which = lax.broadcasted_iota(jnp.int32, (8, 128), 0)
     east = slots_ref[pl.ds(pl.multiple_of(lax.rem(index + 1, devices) * 8, 8), 8)]
@@ -258,8 +260,21 @@
         out_shape=[jax.ShapeDtypeStruct(shape, jnp.float32) for shape in outs],
         scratch_shapes=[pltpu.VMEM(shape, jnp.float32) for shape in scratch],
         compiler_params=pltpu.CompilerParams(vmem_limit_bytes=4 * 2**20),
-        name=kernel.__name__,
+        name=getattr(kernel, "func", kernel).__name__,
     )(*args)
+
+
+def far_first(axes):
+    sizes = [lax.axis_size(axis) for axis in axes]
+
+    def near(member):
+        hops = 0
+        for size in reversed(sizes):
+            hops += min(member % size, size - member % size)
+            member //= size
+        return hops
+
+    return sorted(range(math.prod(sizes)), key=lambda member: (-near(member), member))
 
 
 def local(heat, conduct, spacing, wet, water, depth):
@@ -267,6 +282,9 @@
     tall, wide = rows + 2 * HALO, cols + 128
     ring = lax.axis_size(COL)
     index = lax.axis_index(COL).astype(jnp.int32).reshape(1)
+    order = far_first(COL)
+    over_cols = [[row * ring + col for col in order] for row in range(lax.axis_size(ROW))]
+    over_rows = [[row * ring + col for row in far_first(ROW)] for col in range(ring)]
     diffused, forcing, to_north, to_south = mix(heat, conduct, spacing, wet, water, depth)
     down = [(i, i + 1) for i in range(lax.axis_size(ROW) - 1)]
     north = lax.ppermute(to_south, ROW, down)
@@ -274,13 +292,13 @@
     fields, slots = call(
         edge_kernel, [(3, tall, cols), (ring * 8, 128)], forcing, depth, water, north, south, scratch=[(128, 128)]
     )
-    slots = lax.all_to_all(slots, COL, 0, 0, tiled=True)
+    slots = lax.all_to_all(slots, ROW + COL, 0, 0, axis_index_groups=over_cols, tiled=True)
     full, centre, bound = call(
-        weights_kernel,
+        functools.partial(weights_kernel, order),
         [(3, tall, wide), (tall, wide), (lax.axis_size(ROW), 128)],
-        index, slots, fields, scratch=[(128, 128)],
+        index, slots, fields, scratch=[(128, 128), (ring * 8, 128)],
     )
-    bounds = lax.all_to_all(bound, ROW, 0, 0, tiled=True)
+    bounds = lax.all_to_all(bound, ROW + COL, 0, 0, axis_index_groups=over_rows, tiled=True)
     (height,) = call(solve_kernel, [(rows, cols)], bounds, full, centre)
     return diffused, height
 

time: 72.8 us -> 62.4 us (0.86)
  blocking collectives: 31.5 us -> 22 us
  waiting for transfers between devices: 11.2 us -> 6.33 us
  starting transfers between devices: 21.1 us -> 24.4 us
    all_to_all x1, blocking collectives: 31.5 us -> 22 us  [local(): lax.all_to_all(bound, ROW + COL, 0, 0, axis_index_groups=over_rows, tiled...]
    all_to_all x1, waiting for transfers between devices: 7.82 us -> 2.94 us  [local(): lax.all_to_all(slots, ROW + COL, 0, 0, axis_index_groups=over_cols, tiled...]
    all_to_all x1, starting transfers between devices: 15.9 us -> 19.2 us  [local(): lax.all_to_all(slots, ROW + COL, 0, 0, axis_index_groups=over_cols, tiled...]
where the time goes in v3:
time: 62.4 us; the launch traced here: 61.3 us
  starting transfers between devices  24.4 us (39%)
  blocking collectives  22 us (35%)
  Pallas kernels  7.16 us (11%)
  waiting for transfers between devices  6.33 us (10%)
  local copies, waits for them, and re-layouts  0.77 us (1%)
  between operations  0.68 us (1%)
    all_to_all x1, blocking collectives, local(): lax.all_to_all(bound, ROW + COL, 0, 0, axis_index_groups=over_rows, tiled...  22 us
    all_to_all x1, starting transfers between devices, local(): lax.all_to_all(slots, ROW + COL, 0, 0, axis_index_groups=over_cols, tiled...  19.2 us
    pallas_call x1, Pallas kernels, mix(): pl.pallas_call(mix_kernel, in_specs=[pl.BlockSpec(memory_space=pltpu.SMEM...  4.61 us
    ppermute x1, starting transfers between devices, local(): north = lax.ppermute(to_south, ROW, down)  3.93 us
    ppermute x1, waiting for transfers between devices, local(): south = lax.ppermute(to_north, ROW, [(b, a) for a, b in down])  3.38 us
    all_to_all x1, waiting for transfers between devices, local(): lax.all_to_all(slots, ROW + COL, 0, 0, axis_index_groups=over_cols, tiled...  2.94 us
    pallas_call x3, Pallas kernels, call(): pl.pallas_call(kernel, in_specs=[SMEM if arg.ndim == 1 else VMEM for arg...  2.56 us
    ppermute x1, starting transfers between devices, local(): south = lax.ppermute(to_north, ROW, [(b, a) for a, b in down])  1.29 us
  transfers between devices with their start and end apart: 3, of which 2 were waited for; matrix products, arithmetic and copies ran while one was open for 0% of the time, Pallas kernels for 0%

profile of v3, /device:TPU:1, one launch (start us, length us, event | category | flops | bytes accessed | tf_op | source)
XLA Modules:
  0.0 61.3 jit_solution(365794888307511375)
XLA Ops:
  0.6 0.0 copy-start.1
  0.6 0.0 copy-start
  0.7 4.6 %mix.1 = (f32[48,32,256]{2,1,0:T(8,128)}, f32[32,256]{1,0:T(8,128)}, f32[12,256]{1,0:T(8,128)}, f32[12,256]{1,0:T(8,128)}) custom-call(f32[48]{0:T(128)} %spacing_ref.1, s32[32,256]{1,0:T(8,128)} %wet_hbm.1, s32[32,256]{1,0:T(8,128)} %water_ref.1, f32[32,256]{1,0:T(8,128)} %depth_ref.1, bf16[48,32,256]{2,1,0:T(8,128)(2,1)} %heat_hbm.1, ...), custom_call_target="tpu_custom_call" | custom-call | tf_op jit(solution)/shard_map/mix/pallas_call | solution.py:128
  5.3 3.9 %collective-permute-start = (f32[12,256]{1,0:T(8,128)}, f32[12,256]{1,0:T(8,128)S(1)}, u32[]{:S(2)}, u32[]{:S(2)}) collective-permute-start(f32[12,256]{1,0:T(8,128)} %get-tuple-element.13), channel_id=1, source_target_pairs={{0,16},{16,32},{32,48},{48,64},{64,80},{80,96},{96,112},{112,128},... | collective-permute-start | bytes 36872 | tf_op jit(solution)/shard_map/ppermute | solution.py:290
  9.2 1.3 %collective-permute-start.1 = (f32[12,256]{1,0:T(8,128)}, f32[12,256]{1,0:T(8,128)S(1)}, u32[]{:S(2)}, u32[]{:S(2)}) collective-permute-start(f32[12,256]{1,0:T(8,128)} %get-tuple-element.14), channel_id=1, source_target_pairs={{16,0},{32,16},{48,32},{64,48},{80,64},{96,80},{112,96},{128,112},... | collective-permute-start | bytes 36872 | tf_op jit(solution)/shard_map/ppermute | solution.py:291
  10.5 0.0 collective-permute-done.north_ref
  10.5 3.4 %collective-permute-done.1.south_ref = f32[12,256]{1,0:T(8,128)S(1)} collective-permute-done((f32[12,256]{1,0:T(8,128)}, f32[12,256]{1,0:T(8,128)S(1)}, u32[]{:S(2)}, u32[]{:S(2)}) %collective-permute-start.1) | collective-permute-done | bytes 12320 | tf_op jit(solution)/shard_map/ppermute | solution.py:291
  13.9 0.0 copy-done.1
  13.9 0.0 copy-done
  13.9 0.0 copy-start.2
  13.9 0.8 %copy-done.2 = f32[32,256]{1,0:T(8,128)S(1)} copy-done((f32[32,256]{1,0:T(8,128)S(1)}, f32[32,256]{1,0:T(8,128)}, u32[]{:S(2)}) %copy-start.2) | copy-done | bytes 32792
  14.7 0.9 %edge_kernel.1 = (f32[3,40,256]{2,1,0:T(8,128)S(1)}, f32[128,128]{1,0:T(8,128)}) custom-call(f32[32,256]{1,0:T(8,128)S(1)} %copy-done.2, f32[32,256]{1,0:T(8,128)S(1)} %copy-done.1, s32[32,256]{1,0:T(8,128)S(1)} %copy-done, f32[12,256]{1,0:T(8,128)S(1)} %collective-permute-done.north_ref, f32[12,256]{1,0:T(8,128)S(1)} %collective-permute-done.1.south_ref), custom_call_target="tpu_custom_call" | custom-call | tf_op jit(solution)/shard_map/edge_kernel/pallas_call | solution.py:256
  15.6 19.2 %all-to-all-start = ((f32[16,8,128]{2,1,0:T(8,128)}), f32[16,8,128]{2,1,0:T(8,128)S(1)}, u32[]{:S(2)}, u32[]{:S(2)}) async-start(f32[16,8,128]{2,1,0:T(8,128)} %bitcast.1), calls=%async_computation | async-start | bytes 131072 | tf_op jit(solution)/shard_map/all_to_all | solution.py:295
  34.7 2.9 %all-to-all-done = f32[16,8,128]{2,1,0:T(8,128)S(1)} async-done(((f32[16,8,128]{2,1,0:T(8,128)}), f32[16,8,128]{2,1,0:T(8,128)S(1)}, u32[]{:S(2)}, u32[]{:S(2)}) %all-to-all-start) | async-done | bytes 65568 | tf_op jit(solution)/shard_map/all_to_all | solution.py:295
  37.7 0.4 weights_kernel.1
  38.1 22.0 %all_to_all.22 = f32[64,1,128]{2,1,0:T(1,128)S(1)} all-to-all(f32[64,1,128]{2,1,0:T(1,128)S(1)} %bitcast.9), channel_id=1, replica_groups={{544,480,528,560,608,416,464,496,512,592,624,672,352,400,432,448,576,65..., dimensions={0} | all-to-all | bytes 65536 | tf_op jit(solution)/shard_map/all_to_all | solution.py:301
  60.1 1.2 %solve_kernel.1 = f32[32,256]{1,0:T(8,128)} custom-call(f32[64,128]{1,0:T(8,128)S(1)} %bitcast.8, f32[3,40,384]{2,1,0:T(8,128)S(1)} %get-tuple-element.18.wide_ref, f32[40,384]{1,0:T(8,128)S(1)} %get-tuple-element.19.centre_ref), custom_call_target="tpu_custom_call" | custom-call | tf_op jit(solution)/shard_map/solve_kernel/pallas_call | solution.py:256
Async XLA Ops:
  0.6 13.3 %copy-start.1 = (f32[32,256]{1,0:T(8,128)S(1)}, f32[32,256]{1,0:T(8,128)}, u32[]{:S(2)}) copy-start(f32[32,256]{1,0:T(8,128)} %depth_ref.1) | copy-start | bytes 98308
  0.6 13.3 %copy-start = (s32[32,256]{1,0:T(8,128)S(1)}, s32[32,256]{1,0:T(8,128)}, u32[]{:S(2)}) copy-start(s32[32,256]{1,0:T(8,128)} %water_ref.1) | copy-start | bytes 98308
  5.3 5.2 %collective-permute-start = (f32[12,256]{1,0:T(8,128)}, f32[12,256]{1,0:T(8,128)S(1)}, u32[]{:S(2)}, u32[]{:S(2)}) collective-permute-start(f32[12,256]{1,0:T(8,128)} %get-tuple-element.13), channel_id=1, source_target_pairs={{0,16},{16,32},{32,48},{48,64},{64,80},{80,96},{96,112},{112,128},... | collective-permute-start | bytes 36872 | tf_op jit(solution)/shard_map/ppermute | solution.py:290
  9.2 4.7 %collective-permute-start.1 = (f32[12,256]{1,0:T(8,128)}, f32[12,256]{1,0:T(8,128)S(1)}, u32[]{:S(2)}, u32[]{:S(2)}) collective-permute-start(f32[12,256]{1,0:T(8,128)} %get-tuple-element.14), channel_id=1, source_target_pairs={{16,0},{32,16},{48,32},{64,48},{80,64},{96,80},{112,96},{128,112},... | collective-permute-start | bytes 36872 | tf_op jit(solution)/shard_map/ppermute | solution.py:291
  13.9 0.8 %copy-start.2 = (f32[32,256]{1,0:T(8,128)S(1)}, f32[32,256]{1,0:T(8,128)}, u32[]{:S(2)}) copy-start(f32[32,256]{1,0:T(8,128)} %get-tuple-element.12.forcing_ref) | copy-start | bytes 98308
  15.6 22.1 %all-to-all-start = ((f32[16,8,128]{2,1,0:T(8,128)}), f32[16,8,128]{2,1,0:T(8,128)S(1)}, u32[]{:S(2)}, u32[]{:S(2)}) async-start(f32[16,8,128]{2,1,0:T(8,128)} %bitcast.1), calls=%async_computation | async-start | bytes 131072 | tf_op jit(solution)/shard_map/all_to_all | solution.py:295

commit v4 on v3

v4 whole, which is shorter than its diff:
```python
import functools
import math

import jax
import jax.numpy as jnp
from jax import lax
from jax.experimental import pallas as pl
from jax.experimental.pallas import tpu as pltpu
from jax.sharding import Mesh
from jax.sharding import PartitionSpec as P


ITERS = 4
CHUNK = 6
ROW = ("row_0", "row_1")
COL = ("col_0", "col_1")
HALO = ITERS
VMEM = pl.BlockSpec(memory_space=pltpu.VMEM)
SMEM = pl.BlockSpec(memory_space=pltpu.SMEM)
surface_term = 0.5


def mix_kernel(
    starts, spacing_ref, wet_hbm, water_hbm, depth_hbm, heat_hbm, conduct_hbm, *refs,
):
    ends = depth_hbm is not None
    out_hbm, forcing_hbm, *refs = refs
    if ends:
        north_hbm, south_hbm, *refs = refs
    forcing_ref, wet_ref, water_ref, heat_buf, conduct_buf, ratio_buf, value_buf, *refs = refs
    plane_sem, forcing_sem, heat_sem, conduct_sem, out_sem, *refs = refs
    blocks, levels, block, _ = heat_buf.shape
    chunks = levels // CHUNK

    def plane(source, target, which):
        return [
            pltpu.make_async_copy(
                source.at[pl.ds(start, block)], target.at[pl.ds(slot * block, block)], plane_sem.at[which, slot]
            )
            for slot, start in enumerate(starts)
        ]

    def fetch(chunk):
        first = chunk * CHUNK
        count = min(CHUNK, levels - 1 - first)
        copies = []
        for slot, start in enumerate(starts):
            lines = pl.ds(start, block)
            copies.append(
                pltpu.make_async_copy(
                    heat_hbm.at[pl.ds(first, CHUNK), lines],
                    heat_buf.at[slot, pl.ds(first, CHUNK)],
                    heat_sem.at[slot, chunk],
                )
            )
            copies.append(
                pltpu.make_async_copy(
                    conduct_hbm.at[pl.ds(first, count), lines],
                    conduct_buf.at[slot, pl.ds(first, count)],
                    conduct_sem.at[slot, chunk],
                )
            )
        return copies

    def flush(chunk):
        first = chunk * CHUNK
        return [
            pltpu.make_async_copy(
                value_buf.at[pl.ds(first, CHUNK), pl.ds(slot * block, block)],
                out_hbm.at[pl.ds(first, CHUNK), pl.ds(start, block)],
                out_sem.at[slot, chunk],
            )
            for slot, start in enumerate(starts)
        ]

    wet_copies = plane(wet_hbm, wet_ref, 0)
    water_copies = plane(water_hbm, water_ref, 1)
    for copy in wet_copies:
        copy.start()
    for chunk in range(chunks):
        for copy in fetch(chunk):
            copy.start()
    for copy in water_copies:
        copy.start()
    if ends:
        depth_ref, north_ref, south_ref, edge_sem = refs
        depth_copies = plane(depth_hbm, depth_ref, 2)
        for copy in depth_copies:
            copy.start()
    for copy in wet_copies:
        copy.wait()
    wet = wet_ref[...]
    zero = jnp.zeros(wet.shape, jnp.float32)

    def joined(buf, level):
        return jnp.concatenate([buf[slot, level].astype(jnp.float32) for slot in range(blocks)], axis=0)

    def down(level, carry, last=False):
        couple_prev, ratio_prev, value_prev = carry
        spacing = spacing_ref[level]
        if last:
            couple = zero
        else:
            couple = jnp.where(level + 1 < wet, joined(conduct_buf, level), 0.0)
        source = spacing * joined(heat_buf, level)
        pivot = spacing + couple_prev + couple - couple_prev * ratio_prev
        inverse = 1.0 / pivot
        ratio = couple * inverse
        value = (source + couple_prev * value_prev) * inverse
        ratio_buf[level] = ratio
        value_buf[level] = value
        return couple, ratio, value

    carry = (zero, zero, zero)
    for chunk in range(chunks):
        for copy in fetch(chunk):
            copy.wait()
        first = chunk * CHUNK
        stop = min(first + CHUNK, levels - 1)
        carry = lax.fori_loop(first, stop, down, carry)
    carry = down(levels - 1, carry, last=True)

    def up(step, carry, first):
        below, total = carry
        level = first + CHUNK - 1 - step
        result = value_buf[level] + ratio_buf[level] * below
        value_buf[level] = result
        total = total + jnp.where(level < wet, spacing_ref[level] * result, 0.0)
        return result, total

    carry = (zero, zero)
    for chunk in reversed(range(chunks)):
        carry = lax.fori_loop(0, CHUNK, functools.partial(up, first=chunk * CHUNK), carry)
        for copy in flush(chunk):
            copy.start()
    for copy in water_copies:
        copy.wait()
    ocean = water_ref[...].astype(jnp.float32)
    forcing = ocean * carry[1] * (1.0 / math.sqrt(levels))
    forcing_ref[...] = forcing
    last = [pltpu.make_async_copy(forcing_ref, forcing_hbm, forcing_sem)]
    if ends:
        for copy in depth_copies:
            copy.wait()
        size = blocks * block
        for slot, field in enumerate((forcing, depth_ref[...], ocean)):
            north_ref[slot * HALO : (slot + 1) * HALO] = field[:HALO]
            south_ref[slot * HALO : (slot + 1) * HALO] = field[size - HALO :]
        last.append(pltpu.make_async_copy(north_ref, north_hbm, edge_sem.at[0]))
        last.append(pltpu.make_async_copy(south_ref, south_hbm, edge_sem.at[1]))
    for copy in last:
        copy.start()
    for chunk in reversed(range(chunks)):
        for copy in flush(chunk):
            copy.wait()
    for copy in last:
        copy.wait()


def first_kernel(starts, spacing, wet, water, depth, heat, conduct, *refs):
    mix_kernel(starts, spacing, wet, water, depth, heat, conduct, *refs)


def second_kernel(starts, spacing, wet, water, heat, conduct, begun, *refs):
    mix_kernel(starts, spacing, wet, water, None, heat, conduct, *refs)


def mix(starts, heat, conduct, spacing, wet, water, depth=None, begun=None):
    levels, rows, cols = heat.shape
    chunks, blocks, block = levels // CHUNK, len(starts), 8
    size = blocks * block
    hbm = pl.BlockSpec(memory_space=pltpu.HBM)
    shape = functools.partial(jax.ShapeDtypeStruct, dtype=jnp.float32)
    outs = [shape((levels, rows, cols)), shape((size, cols))]
    scratch = [
        pltpu.VMEM((size, cols), jnp.float32),
        pltpu.VMEM((size, cols), wet.dtype),
        pltpu.VMEM((size, cols), water.dtype),
        pltpu.VMEM((blocks, levels, block, cols), heat.dtype),
        pltpu.VMEM((blocks, levels, block, cols), conduct.dtype),
        pltpu.VMEM((levels, size, cols), jnp.float32),
        pltpu.VMEM((levels, size, cols), jnp.float32),
        pltpu.SemaphoreType.DMA((3, blocks)),
        pltpu.SemaphoreType.DMA,
        pltpu.SemaphoreType.DMA((blocks, chunks)),
        pltpu.SemaphoreType.DMA((blocks, chunks)),
        pltpu.SemaphoreType.DMA((blocks, chunks)),
    ]
    if begun is None:
        outs += [shape((3 * HALO, cols))] * 2
        scratch += [
            pltpu.VMEM((size, cols), depth.dtype),
            pltpu.VMEM((3 * HALO, cols), jnp.float32),
            pltpu.VMEM((3 * HALO, cols), jnp.float32),
            pltpu.SemaphoreType.DMA((2,)),
        ]
        kernel, args, aliases = first_kernel, (spacing, wet, water, depth, heat, conduct), {}
    else:
        kernel, args, aliases = second_kernel, (spacing, wet, water, heat, conduct, begun), {5: 0}
    return pl.pallas_call(
        functools.partial(kernel, starts),
        in_specs=[SMEM] + [hbm] * (len(args) - 1),
        out_specs=[hbm] * len(outs),
        out_shape=outs,
        scratch_shapes=scratch,
        input_output_aliases=aliases,
    )(*args)


def around(field):
    tall, wide = field.shape
    beside = pltpu.roll(field, 1, 0) + pltpu.roll(field, tall - 1, 0)
    slant = field + 0.5 * beside
    return beside + (pltpu.roll(slant, 1, 1) + pltpu.roll(slant, wide - 1, 1))


def centre_of(wet_depth, ocean):
    return surface_term + 0.5 * (wet_depth * around(ocean) + ocean * around(wet_depth))


def most(field):
    return jnp.max(jnp.max(field, axis=0, keepdims=True), axis=1, keepdims=True)


def edge_kernel(outer_ref, depth_ref, water_ref, north_ref, south_ref, tall_ref, slots_ref, pack_ref):
    rows, cols = depth_ref.shape
    tall = rows + 2 * HALO

    def outer(field):
        low = lax.broadcasted_iota(jnp.int32, (field.shape[0], 128), 1) < 64
        return jnp.where(low, field[:, :128], field[:, cols - 128 :])

    pack_ref[:HALO] = outer(north_ref[:HALO])
    pack_ref[HALO : HALO + rows] = outer_ref[...]
    pack_ref[HALO + rows : tall] = outer(south_ref[:HALO])
    for slot, field in enumerate((depth_ref[...], water_ref[...].astype(jnp.float32))):
        tall_ref[slot, :HALO] = north_ref[(slot + 1) * HALO : (slot + 2) * HALO]
        tall_ref[slot, HALO : HALO + rows] = field
        tall_ref[slot, HALO + rows :] = south_ref[(slot + 1) * HALO : (slot + 2) * HALO]
        pack_ref[(slot + 1) * tall : (slot + 2) * tall] = outer(tall_ref[slot])
    ocean = tall_ref[1]
    centre = centre_of(tall_ref[0] * ocean, ocean)
    row = lax.broadcasted_iota(jnp.int32, (tall, cols), 0)
    col = lax.broadcasted_iota(jnp.int32, (tall, cols), 1)
    inner = (row >= HALO) & (row < HALO + rows) & (col >= 1) & (col < cols - 1)
    pack_ref[3 * tall :] = jnp.broadcast_to(most(jnp.where(inner, centre, 0.0)), (128 - 3 * tall, 128))
    turned = pack_ref[...].T
    which = lax.broadcasted_iota(jnp.int32, (8, 128), 0)
    tile = jnp.where(which < HALO, turned[:8], turned[120:])
    for slot in range(slots_ref.shape[0] // 8):
        slots_ref[slot * 8 : (slot + 1) * 8] = tile


def weights_kernel(
    order, index_ref, sent_ref, forcing_ref, north_ref, south_ref, tall_ref,
    wide_ref, centre_ref, bound_ref, pack_ref, slots_ref, forced_ref,
):
    tall, _ = tall_ref.shape[1:]
    rows = tall - 2 * HALO
    forced_ref[:HALO] = north_ref[:HALO]
    forced_ref[HALO : HALO + rows] = forcing_ref[...]
    forced_ref[HALO + rows :] = south_ref[:HALO]
    devices = len(order)
    for slot, device in enumerate(order):
        slots_ref[device * 8 : (device + 1) * 8] = sent_ref[slot * 8 : (slot + 1) * 8]
    index = index_ref[0]
    which = lax.broadcasted_iota(jnp.int32, (8, 128), 0)
    east = slots_ref[pl.ds(pl.multiple_of(lax.rem(index + 1, devices) * 8, 8), 8)]
    west = slots_ref[pl.ds(pl.multiple_of(lax.rem(index + devices - 1, devices) * 8, 8), 8)]
    pack_ref[...] = jnp.zeros((128, 128), jnp.float32)
    pack_ref[:8] = jnp.where(which < HALO, east, 0.0)
    pack_ref[120:] = jnp.where(which >= HALO, west, 0.0)
    turned = pack_ref[...].T
    forcing, depth, ocean = (
        jnp.concatenate([field, turned[slot * tall : (slot + 1) * tall]], axis=1)
        for slot, field in enumerate((forced_ref[...], tall_ref[0], tall_ref[1]))
    )
    wet_depth = depth * ocean
    wide_ref[0] = forcing
    wide_ref[1] = wet_depth
    wide_ref[2] = ocean
    centre_ref[...] = centre_of(wet_depth, ocean)
    slots = slots_ref[...]
    joint = pltpu.roll(slots, HALO, 0)
    joint_ocean = pltpu.roll(joint, 128 - tall, 1)
    joint_centre = centre_of(joint * joint_ocean, joint_ocean)
    row = lax.broadcasted_iota(jnp.int32, joint.shape, 0) % 8
    lane = lax.broadcasted_iota(jnp.int32, joint.shape, 1)
    seam = ((row == HALO - 1) | (row == HALO)) & (lane >= tall + HALO) & (lane < 2 * tall - HALO)
    high = most(jnp.where(seam, joint_centre, jnp.where(lane >= 3 * tall, slots, 0.0)))
    bound_ref[...] = jnp.broadcast_to(high, bound_ref.shape)


def solve_kernel(bounds_ref, wide_ref, centre_ref, height_ref):
    rows, cols = height_ref.shape
    _, wide = centre_ref.shape
    top = 2.0 * jnp.max(bounds_ref[...], axis=0, keepdims=True) - surface_term
    top = jnp.concatenate([top] * (wide // 128), axis=1)
    theta = 0.5 * (top + surface_term)
    delta = 0.5 * (top - surface_term)
    sigma = theta / delta
    wet_depth, ocean, centre = wide_ref[1], wide_ref[2], centre_ref[...]
    residual = wide_ref[0]
    direction = residual / theta
    total = direction
    recur = 1.0 / sigma
    for _ in range(ITERS):
        image = centre * direction - 0.5 * (
            wet_depth * around(ocean * direction) + ocean * around(wet_depth * direction)
        )
        residual = residual - image
        recur_next = 1.0 / (2.0 * sigma - recur)
        direction = (recur_next * recur) * direction + (2.0 * recur_next / delta) * residual
        recur = recur_next
        total = total + direction
    height_ref[...] = total[HALO : HALO + rows, :cols]


def call(kernel, outs, *args, scratch=()):
    return pl.pallas_call(
        kernel,
        in_specs=[SMEM if arg.ndim == 1 else VMEM for arg in args],
        out_specs=[VMEM] * len(outs),
        out_shape=[jax.ShapeDtypeStruct(shape, jnp.float32) for shape in outs],
        scratch_shapes=[pltpu.VMEM(shape, jnp.float32) for shape in scratch],
        compiler_params=pltpu.CompilerParams(vmem_limit_bytes=4 * 2**20),
    )(*args)


def far_first(axes):
    sizes = [lax.axis_size(axis) for axis in axes]

    def near(member):
        hops = 0
        for size in reversed(sizes):
            hops += min(member % size, size - member % size)
            member //= size
        return hops

    return sorted(range(math.prod(sizes)), key=lambda member: (-near(member), member))


def step(heat, conduct, spacing, wet, water, depth):
    rows, cols = depth.shape
    tall, wide = rows + 2 * HALO, cols + 128
    ring = lax.axis_size(COL)
    index = lax.axis_index(COL).astype(jnp.int32).reshape(1)
    order = far_first(COL)
    over_cols = [[row * ring + col for col in order] for row in range(lax.axis_size(ROW))]
    over_rows = [[row * ring + col for row in far_first(ROW)] for col in range(ring)]
    blocks = list(range(0, rows, 8))
    outside, inside = [blocks[0], blocks[-1]], blocks[1:-1]
    diffused, forcing_ends, to_north, to_south = mix(outside, heat, conduct, spacing, wet, water, depth=depth)
    down = [(i, i + 1) for i in range(lax.axis_size(ROW) - 1)]
    north = lax.ppermute(to_south, ROW, down)
    south = lax.ppermute(to_north, ROW, [(b, a) for a, b in down])
    diffused, forcing_inside = mix(inside, heat, conduct, spacing, wet, water, begun=diffused)
    forcing = jnp.concatenate([forcing_ends[:8], forcing_inside, forcing_ends[8:]])
    low = lax.broadcasted_iota(jnp.int32, (rows, 128), 1) < 64
    outer = jnp.where(low, forcing[:, :128], forcing[:, cols - 128 :])
    fields, slots = call(
        edge_kernel, [(2, tall, cols), (ring * 8, 128)], outer, depth, water, north, south, scratch=[(128, 128)]
    )
    slots = lax.all_to_all(slots, ROW + COL, 0, 0, axis_index_groups=over_cols, tiled=True)
    full, centre, bound = call(
        functools.partial(weights_kernel, order),
        [(3, tall, wide), (tall, wide), (lax.axis_size(ROW), 128)],
        index, slots, forcing, north, south, fields, scratch=[(128, 128), (ring * 8, 128), (tall, cols)],
    )
    bounds = lax.all_to_all(bound, ROW + COL, 0, 0, axis_index_groups=over_rows, tiled=True)
    (height,) = call(solve_kernel, [(rows, cols)], bounds, full, centre)
    return diffused, height


def solution(mesh):
    torus = Mesh(mesh.devices.reshape(16, 4, 8, 2), ROW + COL)
    return jax.shard_map(
        step,
        mesh=torus,
        in_specs=(P(None, ROW, COL), P(None, ROW, COL), P(), P(ROW, COL), P(ROW, COL), P(ROW, COL)),
        out_specs=(P(None, ROW, COL), P(ROW, COL)),
        check_vma=False,
    )
```

time: 62.4 us -> 63.2 us (1.013)
  Pallas kernels: 7.16 us -> 10.9 us
  waiting for transfers between devices: 6.33 us -> 2.95 us
  blocking collectives: 22 us -> 23.7 us
  starting transfers between devices: 24.4 us -> 23.2 us
  local copies, waits for them, and re-layouts: 0.77 us -> 0.02 us
  other arithmetic: 0 us -> 0.73 us
    pallas_call x1 -> x2, Pallas kernels: 4.61 us -> 8.31 us  [mix(): pl.pallas_call(functools.partial(kernel, starts), in_specs=[SMEM] + [hbm]...]
    ppermute x2, waiting for transfers between devices: 3.39 us -> 0.01 us  [the longest x1 0.01 us: step(): south = lax.ppermute(to_north, ROW, [(b, a) for a, b in down])]
    all_to_all x1, blocking collectives: 22 us -> 23.7 us  [step(): lax.all_to_all(bound, ROW + COL, 0, 0, axis_index_groups=over_rows, tiled...]
    all_to_all x1, starting transfers between devices: 19.2 us -> 18 us  [step(): lax.all_to_all(slots, ROW + COL, 0, 0, axis_index_groups=over_cols, tiled...]
    unnamed x6, local copies, waits for them, and re-layouts: 0.77 us -> 0.02 us
    concatenate x0 -> x1, other arithmetic: none -> 0.72 us  [step(): jnp.concatenate([forcing_ends[:8], forcing_inside, forcing_ends[8:]])]
  transfers between devices with their start and end apart: 3 -> 3, of which waited for: 2 -> 1; matrix products, arithmetic and copies ran while one was open for 0% -> 1% of each run, Pallas kernels for 0% -> 7%
where the time goes in v4:
time: 63.2 us; the launch traced here: 62.3 us
  blocking collectives  23.7 us (38%)
  starting transfers between devices  23.2 us (37%)
  Pallas kernels  10.9 us (17%)
  waiting for transfers between devices  2.95 us (5%)
  other arithmetic  0.73 us (1%)
  between operations  0.73 us (1%)
    all_to_all x1, blocking collectives, step(): lax.all_to_all(bound, ROW + COL, 0, 0, axis_index_groups=over_rows, tiled...  23.7 us
    all_to_all x1, starting transfers between devices, step(): lax.all_to_all(slots, ROW + COL, 0, 0, axis_index_groups=over_cols, tiled...  18 us
    pallas_call x2, Pallas kernels, mix(): pl.pallas_call(functools.partial(kernel, starts), in_specs=[SMEM] + [hbm]...  8.31 us
    ppermute x1, starting transfers between devices, step(): north = lax.ppermute(to_south, ROW, down)  3.93 us
    all_to_all x1, waiting for transfers between devices, step(): lax.all_to_all(slots, ROW + COL, 0, 0, axis_index_groups=over_cols, tiled...  2.94 us
    pallas_call x3, Pallas kernels, call(): pl.pallas_call(kernel, in_specs=[SMEM if arg.ndim == 1 else VMEM for arg...  2.56 us
    ppermute x1, starting transfers between devices, step(): south = lax.ppermute(to_north, ROW, [(b, a) for a, b in down])  1.29 us
  transfers between devices with their start and end apart: 3, of which 1 were waited for; matrix products, arithmetic and copies ran while one was open for 1% of the time, Pallas kernels for 7%

profile of v4, /device:TPU:1, one launch (start us, length us, event | category | flops | bytes accessed | tf_op | source)
XLA Modules:
  0.0 62.3 jit_solution(12907852245573549918)
XLA Ops:
  0.6 4.1 %shard_map.77 = (f32[48,32,256]{2,1,0:T(8,128)}, f32[16,256]{1,0:T(8,128)}, f32[12,256]{1,0:T(8,128)}, f32[12,256]{1,0:T(8,128)}) custom-call(f32[48]{0:T(128)} %spacing.3, s32[32,256]{1,0:T(8,128)} %wet.3, s32[32,256]{1,0:T(8,128)} %water_ref.1, f32[32,256]{1,0:T(8,128)} %depth_ref.1, bf16[48,32,256]{2,1,0:T(8,128)(2,1)} %heat.3, bf16[47,32,256]{2,1,0:T(8,128)(2,1)} %conduct.3), custom_call_target="tpu_custom_call" | custom-call | tf_op jit(solution)/shard_map/pallas_call | solution.py:200
  4.7 3.9 %collective-permute-start = (f32[12,256]{1,0:T(8,128)}, f32[12,256]{1,0:T(8,128)S(1)}, u32[]{:S(2)}, u32[]{:S(2)}) collective-permute-start(f32[12,256]{1,0:T(8,128)} %get-tuple-element.17), channel_id=1, source_target_pairs={{0,16},{16,32},{32,48},{48,64},{64,80},{80,96},{96,112},{112,128},... | collective-permute-start | bytes 36872 | tf_op jit(solution)/shard_map/ppermute | solution.py:355
  8.7 1.3 %collective-permute-start.1 = (f32[12,256]{1,0:T(8,128)}, f32[12,256]{1,0:T(8,128)S(1)}, u32[]{:S(2)}, u32[]{:S(2)}) collective-permute-start(f32[12,256]{1,0:T(8,128)} %get-tuple-element.18), channel_id=1, source_target_pairs={{16,0},{32,16},{48,32},{64,48},{80,64},{96,80},{112,96},{128,112},... | collective-permute-start | bytes 36872 | tf_op jit(solution)/shard_map/ppermute | solution.py:356
  10.0 0.0 copy-start.2
  10.0 0.0 copy-start
  10.0 0.0 copy-start.1
  10.0 4.2 %shard_map.78 = (f32[48,32,256]{2,1,0:T(8,128)}, f32[16,256]{1,0:T(8,128)}) custom-call(f32[48]{0:T(128)} %spacing.3, s32[32,256]{1,0:T(8,128)} %wet.3, s32[32,256]{1,0:T(8,128)} %water_ref.1, bf16[48,32,256]{2,1,0:T(8,128)(2,1)} %heat.3, bf16[47,32,256]{2,1,0:T(8,128)(2,1)} %conduct.3, ...), custom_call_target="tpu_custom_call", output_to_operand_aliasing={{0}: (5, {})} | custom-call | tf_op jit(solution)/shard_map/pallas_call | solution.py:200
  14.2 0.0 copy-done.2
  14.3 0.7 %pad_maximum_fusion.forcing_ref = f32[32,256]{1,0:T(8,128)S(1)} fusion(f32[8,256]{1,0:T(8,128)S(1)} %get-tuple-element.25, f32[16,256]{1,0:T(8,128)} %get-tuple-element.16, f32[8,256]{1,0:T(8,128)S(1)} %get-tuple-element.24), kind=kLoop, calls=%fused_computation | loop fusion | flops 16384 | bytes 65536 | tf_op jit(solution)/shard_map/concatenate | solution.py:358
  15.0 0.0 collective-permute-done.north_ref
  15.0 0.0 collective-permute-done.1.south_ref
  15.0 0.0 copy-done
  15.0 0.0 copy-done.1
  15.0 0.9 %shard_map.79 = (f32[2,40,256]{2,1,0:T(8,128)S(1)}, f32[128,128]{1,0:T(8,128)}) custom-call(f32[32,128]{1,0:T(8,128)S(1)} %slice_select_fusion.outer_ref, f32[32,256]{1,0:T(8,128)S(1)} %copy-done.1, s32[32,256]{1,0:T(8,128)S(1)} %copy-done, f32[12,256]{1,0:T(8,128)S(1)} %collective-permute-done.north_ref, f32[12,256]{1,0:T(8,128)S(1)} %collective-permute-done.1.south_ref), custom_call_target="tpu_custom_call" | custom-call | tf_op jit(solution)/shard_map/pallas_call | solution.py:320
  15.9 18.0 %all-to-all-start = ((f32[16,8,128]{2,1,0:T(8,128)}), f32[16,8,128]{2,1,0:T(8,128)S(1)}, u32[]{:S(2)}, u32[]{:S(2)}) async-start(f32[16,8,128]{2,1,0:T(8,128)} %bitcast.1), calls=%async_computation | async-start | bytes 131072 | tf_op jit(solution)/shard_map/all_to_all | solution.py:364
  34.0 2.9 %all-to-all-done = f32[16,8,128]{2,1,0:T(8,128)S(1)} async-done(((f32[16,8,128]{2,1,0:T(8,128)}), f32[16,8,128]{2,1,0:T(8,128)S(1)}, u32[]{:S(2)}, u32[]{:S(2)}) %all-to-all-start) | async-done | bytes 65568 | tf_op jit(solution)/shard_map/all_to_all | solution.py:364
  36.9 0.4 shard_map.80
  37.3 23.7 %all_to_all.22 = f32[64,1,128]{2,1,0:T(1,128)S(1)} all-to-all(f32[64,1,128]{2,1,0:T(1,128)S(1)} %bitcast.9), channel_id=1, replica_groups={{544,480,528,560,608,416,464,496,512,592,624,672,352,400,432,448,576,65..., dimensions={0} | all-to-all | bytes 65536 | tf_op jit(solution)/shard_map/all_to_all | solution.py:370
  61.0 1.2 %shard_map.81 = f32[32,256]{1,0:T(8,128)} custom-call(f32[64,128]{1,0:T(8,128)S(1)} %bitcast.8, f32[3,40,384]{2,1,0:T(8,128)S(1)} %get-tuple-element.22.wide_ref, f32[40,384]{1,0:T(8,128)S(1)} %get-tuple-element.23.centre_ref), custom_call_target="tpu_custom_call" | custom-call | tf_op jit(solution)/shard_map/pallas_call | solution.py:320
  (3 shorter events, 0.0 us)
Async XLA Ops:
  4.7 10.3 %collective-permute-start = (f32[12,256]{1,0:T(8,128)}, f32[12,256]{1,0:T(8,128)S(1)}, u32[]{:S(2)}, u32[]{:S(2)}) collective-permute-start(f32[12,256]{1,0:T(8,128)} %get-tuple-element.17), channel_id=1, source_target_pairs={{0,16},{16,32},{32,48},{48,64},{64,80},{80,96},{96,112},{112,128},... | collective-permute-start | bytes 36872 | tf_op jit(solution)/shard_map/ppermute | solution.py:355
  8.7 6.3 %collective-permute-start.1 = (f32[12,256]{1,0:T(8,128)}, f32[12,256]{1,0:T(8,128)S(1)}, u32[]{:S(2)}, u32[]{:S(2)}) collective-permute-start(f32[12,256]{1,0:T(8,128)} %get-tuple-element.18), channel_id=1, source_target_pairs={{16,0},{32,16},{48,32},{64,48},{80,64},{96,80},{112,96},{128,112},... | collective-permute-start | bytes 36872 | tf_op jit(solution)/shard_map/ppermute | solution.py:356
  10.0 4.3 %copy-start.2 = (f32[16,256]{1,0:T(8,128)S(1)}, f32[16,256]{1,0:T(8,128)}, u32[]{:S(2)}) copy-start(f32[16,256]{1,0:T(8,128)} %get-tuple-element.15) | copy-start | bytes 49156
  10.0 5.0 %copy-start = (s32[32,256]{1,0:T(8,128)S(1)}, s32[32,256]{1,0:T(8,128)}, u32[]{:S(2)}) copy-start(s32[32,256]{1,0:T(8,128)} %water_ref.1) | copy-start | bytes 98308
  10.0 5.0 %copy-start.1 = (f32[32,256]{1,0:T(8,128)S(1)}, f32[32,256]{1,0:T(8,128)}, u32[]{:S(2)}) copy-start(f32[32,256]{1,0:T(8,128)} %depth_ref.1) | copy-start | bytes 98308
  15.9 21.0 %all-to-all-start = ((f32[16,8,128]{2,1,0:T(8,128)}), f32[16,8,128]{2,1,0:T(8,128)S(1)}, u32[]{:S(2)}, u32[]{:S(2)}) async-start(f32[16,8,128]{2,1,0:T(8,128)} %bitcast.1), calls=%async_computation | async-start | bytes 131072 | tf_op jit(solution)/shard_map/all_to_all | solution.py:364

commit v5 on v3

--- a/solution.py
+++ b/solution.py
@@ -171,19 +171,24 @@
     return jnp.max(jnp.max(field, axis=0, keepdims=True), axis=1, keepdims=True)
 
 
-def edge_kernel(forcing_ref, depth_ref, water_ref, north_ref, south_ref, tall_ref, slots_ref, pack_ref):
-    rows, cols = forcing_ref.shape
+def edge_kernel(outer_ref, depth_ref, water_ref, north_ref, south_ref, tall_ref, slots_ref, pack_ref):
+    rows, cols = depth_ref.shape
     tall = rows + 2 * HALO
-    lane = lax.broadcasted_iota(jnp.int32, (tall, 128), 1)
-    for slot, field in enumerate((forcing_ref[...], depth_ref[...], water_ref[...].astype(jnp.float32))):
-        tall_ref[slot, :HALO] = north_ref[slot * HALO : (slot + 1) * HALO]
+
+    def outer(field):
+        low = lax.broadcasted_iota(jnp.int32, (field.shape[0], 128), 1) < 64
+        return jnp.where(low, field[:, :128], field[:, cols - 128 :])
+
+    pack_ref[:HALO] = outer(north_ref[:HALO])
+    pack_ref[HALO : HALO + rows] = outer_ref[...]
+    pack_ref[HALO + rows : tall] = outer(south_ref[:HALO])
+    for slot, field in enumerate((depth_ref[...], water_ref[...].astype(jnp.float32))):
+        tall_ref[slot, :HALO] = north_ref[(slot + 1) * HALO : (slot + 2) * HALO]
         tall_ref[slot, HALO : HALO + rows] = field
-        tall_ref[slot, HALO + rows :] = south_ref[slot * HALO : (slot + 1) * HALO]
-        pack_ref[slot * tall : (slot + 1) * tall] = jnp.where(
-            lane < 64, tall_ref[slot, :, :128], tall_ref[slot, :, cols - 128 :]
-        )
-    ocean = tall_ref[2]
-    centre = centre_of(tall_ref[1] * ocean, ocean)
+        tall_ref[slot, HALO + rows :] = south_ref[(slot + 1) * HALO : (slot + 2) * HALO]
+        pack_ref[(slot + 1) * tall : (slot + 2) * tall] = outer(tall_ref[slot])
+    ocean = tall_ref[1]
+    centre = centre_of(tall_ref[0] * ocean, ocean)
     row = lax.broadcasted_iota(jnp.int32, (tall, cols), 0)
     col = lax.broadcasted_iota(jnp.int32, (tall, cols), 1)
     inner = (row >= HALO) & (row < HALO + rows) & (col >= 1) & (col < cols - 1)
@@ -195,8 +200,15 @@
         slots_ref[slot * 8 : (slot + 1) * 8] = tile
 
 
-def weights_kernel(order, index_ref, sent_ref, tall_ref, wide_ref, centre_ref, bound_ref, pack_ref, slots_ref):
+def weights_kernel(
+    order, index_ref, sent_ref, forcing_ref, north_ref, south_ref, tall_ref,
+    wide_ref, centre_ref, bound_ref, pack_ref, slots_ref, forced_ref,
+):
     tall, cols = tall_ref.shape[1:]
+    rows = tall - 2 * HALO
+    forced_ref[:HALO] = north_ref[:HALO]
+    forced_ref[HALO : HALO + rows] = forcing_ref[...]
+    forced_ref[HALO + rows :] = south_ref[:HALO]
     devices = len(order)
     for slot, device in enumerate(order):
         slots_ref[device * 8 : (device + 1) * 8] = sent_ref[slot * 8 : (slot + 1) * 8]
@@ -209,7 +221,8 @@
     pack_ref[120:] = jnp.where(which >= HALO, west, 0.0)
     turned = pack_ref[...].T
     forcing, depth, ocean = (
-        jnp.concatenate([tall_ref[slot], turned[slot * tall : (slot + 1) * tall]], axis=1) for slot in range(3)
+        jnp.concatenate([field, turned[slot * tall : (slot + 1) * tall]], axis=1)
+        for slot, field in enumerate((forced_ref[...], tall_ref[0], tall_ref[1]))
     )
     wet_depth = depth * ocean
     wide_ref[0] = forcing
@@ -289,14 +302,16 @@
     down = [(i, i + 1) for i in range(lax.axis_size(ROW) - 1)]
     north = lax.ppermute(to_south, ROW, down)
     south = lax.ppermute(to_north, ROW, [(b, a) for a, b in down])
+    low = lax.broadcasted_iota(jnp.int32, (rows, 128), 1) < 64
+    outer = jnp.where(low, forcing[:, :128], forcing[:, cols - 128 :])
     fields, slots = call(
-        edge_kernel, [(3, tall, cols), (ring * 8, 128)], forcing, depth, water, north, south, scratch=[(128, 128)]
+        edge_kernel, [(2, tall, cols), (ring * 8, 128)], outer, depth, water, north, south, scratch=[(128, 128)]
     )
     slots = lax.all_to_all(slots, ROW + COL, 0, 0, axis_index_groups=over_cols, tiled=True)
     full, centre, bound = call(
         functools.partial(weights_kernel, order),
         [(3, tall, wide), (tall, wide), (lax.axis_size(ROW), 128)],
-        index, slots, fields, scratch=[(128, 128), (ring * 8, 128)],
+        index, slots, forcing, north, south, fields, scratch=[(128, 128), (ring * 8, 128), (tall, cols)],
     )
     bounds = lax.all_to_all(bound, ROW + COL, 0, 0, axis_index_groups=over_rows, tiled=True)
     (height,) = call(solve_kernel, [(rows, cols)], bounds, full, centre)

time: 62.4 us -> 62.5 us (level)
  other arithmetic: 0 us -> 0.75 us
  waiting for transfers between devices: 6.33 us -> 5.58 us
    ppermute x1, waiting for transfers between devices: 3.38 us -> 2.64 us  [local(): south = lax.ppermute(to_north, ROW, [(b, a) for a, b in down])]
    select_n x0 -> x1, other arithmetic: none -> 0.74 us  [local(): outer = jnp.where(low, forcing[:, :128], forcing[:, cols - 128:])]
  transfers between devices with their start and end apart: 3 -> 3, of which waited for: 2 -> 2; matrix products, arithmetic and copies ran while one was open for 0% -> 1% of each run, Pallas kernels for 0% -> 0%
where the time goes in v5:
time: 62.5 us; the launch traced here: 61.3 us
  starting transfers between devices  24.4 us (39%)
  blocking collectives  22 us (35%)
  Pallas kernels  7.16 us (11%)
  waiting for transfers between devices  5.58 us (9%)
  local copies, waits for them, and re-layouts  0.77 us (1%)
  other arithmetic  0.75 us (1%)
  between operations  0.68 us (1%)
    all_to_all x1, blocking collectives, local(): lax.all_to_all(bound, ROW + COL, 0, 0, axis_index_groups=over_rows, tiled...  22 us
    all_to_all x1, starting transfers between devices, local(): lax.all_to_all(slots, ROW + COL, 0, 0, axis_index_groups=over_cols, tiled...  19.2 us
    pallas_call x1, Pallas kernels, mix(): pl.pallas_call(mix_kernel, in_specs=[pl.BlockSpec(memory_space=pltpu.SMEM...  4.61 us
    ppermute x1, starting transfers between devices, local(): north = lax.ppermute(to_south, ROW, down)  3.93 us
    all_to_all x1, waiting for transfers between devices, local(): lax.all_to_all(slots, ROW + COL, 0, 0, axis_index_groups=over_cols, tiled...  2.94 us
    ppermute x1, waiting for transfers between devices, local(): south = lax.ppermute(to_north, ROW, [(b, a) for a, b in down])  2.64 us
    pallas_call x3, Pallas kernels, call(): pl.pallas_call(kernel, in_specs=[SMEM if arg.ndim == 1 else VMEM for arg...  2.56 us
    ppermute x1, starting transfers between devices, local(): south = lax.ppermute(to_north, ROW, [(b, a) for a, b in down])  1.29 us
  transfers between devices with their start and end apart: 3, of which 2 were waited for; matrix products, arithmetic and copies ran while one was open for 1% of the time, Pallas kernels for 0%

profile of v5, /device:TPU:1, one launch (start us, length us, event | category | flops | bytes accessed | tf_op | source)
XLA Modules:
  0.0 61.3 jit_solution(971454591116742776)
XLA Ops:
  0.6 0.0 copy-start.1
  0.6 0.0 copy-start
  0.7 4.6 %mix.1 = (f32[48,32,256]{2,1,0:T(8,128)}, f32[32,256]{1,0:T(8,128)}, f32[12,256]{1,0:T(8,128)}, f32[12,256]{1,0:T(8,128)}) custom-call(f32[48]{0:T(128)} %spacing_ref.1, s32[32,256]{1,0:T(8,128)} %wet_hbm.1, s32[32,256]{1,0:T(8,128)} %water_ref.1, f32[32,256]{1,0:T(8,128)} %depth_ref.1, bf16[48,32,256]{2,1,0:T(8,128)(2,1)} %heat_hbm.1, ...), custom_call_target="tpu_custom_call" | custom-call | tf_op jit(solution)/shard_map/mix/pallas_call | solution.py:128
  5.3 3.9 %collective-permute-start = (f32[12,256]{1,0:T(8,128)}, f32[12,256]{1,0:T(8,128)S(1)}, u32[]{:S(2)}, u32[]{:S(2)}) collective-permute-start(f32[12,256]{1,0:T(8,128)} %get-tuple-element.13), channel_id=1, source_target_pairs={{0,16},{16,32},{32,48},{48,64},{64,80},{80,96},{96,112},{112,128},... | collective-permute-start | bytes 36872 | tf_op jit(solution)/shard_map/ppermute | solution.py:303
  9.2 1.3 %collective-permute-start.1 = (f32[12,256]{1,0:T(8,128)}, f32[12,256]{1,0:T(8,128)S(1)}, u32[]{:S(2)}, u32[]{:S(2)}) collective-permute-start(f32[12,256]{1,0:T(8,128)} %get-tuple-element.14), channel_id=1, source_target_pairs={{16,0},{32,16},{48,32},{64,48},{80,64},{96,80},{112,96},{128,112},... | collective-permute-start | bytes 36872 | tf_op jit(solution)/shard_map/ppermute | solution.py:304
  10.5 0.7 %slice_select_fusion.outer_ref = f32[32,128]{1,0:T(8,128)S(1)} fusion(f32[32,256]{1,0:T(8,128)} %get-tuple-element.12.forcing_ref, pred[128]{0:T(512)(128)(4,1)S(1)} %iota_compare_fusion), kind=kLoop, calls=%fused_computation | loop fusion | flops 4096 | bytes 49280 | tf_op jit(solution)/shard_map/jit(_where)/select_n | solution.py:306
  11.3 0.0 collective-permute-done.north_ref
  11.3 2.6 %collective-permute-done.1.south_ref = f32[12,256]{1,0:T(8,128)S(1)} collective-permute-done((f32[12,256]{1,0:T(8,128)}, f32[12,256]{1,0:T(8,128)S(1)}, u32[]{:S(2)}, u32[]{:S(2)}) %collective-permute-start.1) | collective-permute-done | bytes 12320 | tf_op jit(solution)/shard_map/ppermute | solution.py:304
  13.9 0.0 copy-done.1
  13.9 0.0 copy-done
  13.9 0.9 %edge_kernel.1 = (f32[2,40,256]{2,1,0:T(8,128)S(1)}, f32[128,128]{1,0:T(8,128)}) custom-call(f32[32,128]{1,0:T(8,128)S(1)} %slice_select_fusion.outer_ref, f32[32,256]{1,0:T(8,128)S(1)} %copy-done.1, s32[32,256]{1,0:T(8,128)S(1)} %copy-done, f32[12,256]{1,0:T(8,128)S(1)} %collective-permute-done.north_ref, f32[12,256]{1,0:T(8,128)S(1)} %collective-permute-done.1.south_ref), custom_call_target="tpu_custom_call" | custom-call | tf_op jit(solution)/shard_map/edge_kernel/pallas_call | solution.py:269
  14.8 19.2 %all-to-all-start = ((f32[16,8,128]{2,1,0:T(8,128)}), f32[16,8,128]{2,1,0:T(8,128)S(1)}, u32[]{:S(2)}, u32[]{:S(2)}) async-start(f32[16,8,128]{2,1,0:T(8,128)} %bitcast.1), calls=%async_computation | async-start | bytes 131072 | tf_op jit(solution)/shard_map/all_to_all | solution.py:310
  34.0 2.9 %all-to-all-done = f32[16,8,128]{2,1,0:T(8,128)S(1)} async-done(((f32[16,8,128]{2,1,0:T(8,128)}), f32[16,8,128]{2,1,0:T(8,128)S(1)}, u32[]{:S(2)}, u32[]{:S(2)}) %all-to-all-start) | async-done | bytes 65568 | tf_op jit(solution)/shard_map/all_to_all | solution.py:310
  36.9 0.0 copy-start.2
  36.9 0.8 %copy-done.2 = f32[32,256]{1,0:T(8,128)S(1)} copy-done((f32[32,256]{1,0:T(8,128)S(1)}, f32[32,256]{1,0:T(8,128)}, u32[]{:S(2)}) %copy-start.2) | copy-done | bytes 32792
  37.7 0.4 weights_kernel.1
  38.1 22.0 %all_to_all.22 = f32[64,1,128]{2,1,0:T(1,128)S(1)} all-to-all(f32[64,1,128]{2,1,0:T(1,128)S(1)} %bitcast.9), channel_id=1, replica_groups={{544,480,528,560,608,416,464,496,512,592,624,672,352,400,432,448,576,65..., dimensions={0} | all-to-all | bytes 65536 | tf_op jit(solution)/shard_map/all_to_all | solution.py:316
  60.1 1.2 %solve_kernel.1 = f32[32,256]{1,0:T(8,128)} custom-call(f32[64,128]{1,0:T(8,128)S(1)} %bitcast.8, f32[3,40,384]{2,1,0:T(8,128)S(1)} %get-tuple-element.18.wide_ref, f32[40,384]{1,0:T(8,128)S(1)} %get-tuple-element.19.centre_ref), custom_call_target="tpu_custom_call" | custom-call | tf_op jit(solution)/shard_map/solve_kernel/pallas_call | solution.py:269
  (1 shorter events, 0.0 us)
Async XLA Ops:
  0.6 13.3 %copy-start.1 = (f32[32,256]{1,0:T(8,128)S(1)}, f32[32,256]{1,0:T(8,128)}, u32[]{:S(2)}) copy-start(f32[32,256]{1,0:T(8,128)} %depth_ref.1) | copy-start | bytes 98308
  0.6 13.3 %copy-start = (s32[32,256]{1,0:T(8,128)S(1)}, s32[32,256]{1,0:T(8,128)}, u32[]{:S(2)}) copy-start(s32[32,256]{1,0:T(8,128)} %water_ref.1) | copy-start | bytes 98308
  5.3 6.0 %collective-permute-start = (f32[12,256]{1,0:T(8,128)}, f32[12,256]{1,0:T(8,128)S(1)}, u32[]{:S(2)}, u32[]{:S(2)}) collective-permute-start(f32[12,256]{1,0:T(8,128)} %get-tuple-element.13), channel_id=1, source_target_pairs={{0,16},{16,32},{32,48},{48,64},{64,80},{80,96},{96,112},{112,128},... | collective-permute-start | bytes 36872 | tf_op jit(solution)/shard_map/ppermute | solution.py:303
  9.2 4.7 %collective-permute-start.1 = (f32[12,256]{1,0:T(8,128)}, f32[12,256]{1,0:T(8,128)S(1)}, u32[]{:S(2)}, u32[]{:S(2)}) collective-permute-start(f32[12,256]{1,0:T(8,128)} %get-tuple-element.14), channel_id=1, source_target_pairs={{16,0},{32,16},{48,32},{64,48},{80,64},{96,80},{112,96},{128,112},... | collective-permute-start | bytes 36872 | tf_op jit(solution)/shard_map/ppermute | solution.py:304
  14.8 22.1 %all-to-all-start = ((f32[16,8,128]{2,1,0:T(8,128)}), f32[16,8,128]{2,1,0:T(8,128)S(1)}, u32[]{:S(2)}, u32[]{:S(2)}) async-start(f32[16,8,128]{2,1,0:T(8,128)} %bitcast.1), calls=%async_computation | async-start | bytes 131072 | tf_op jit(solution)/shard_map/all_to_all | solution.py:310
  36.9 0.8 %copy-start.2 = (f32[32,256]{1,0:T(8,128)S(1)}, f32[32,256]{1,0:T(8,128)}, u32[]{:S(2)}) copy-start(f32[32,256]{1,0:T(8,128)} %get-tuple-element.12.forcing_ref) | copy-start | bytes 98308
